TPU v7x, 128 devices: a whole 4x4x4 slice. The times are simulated.
128 devices in a mesh: tm: 16 (over x, y), series: 8 (over z, core).
Axes of the slice: x: 4, y: 4, z: 4, core: 2. Of those that a mesh axis runs over, the one named last changes fastest.
Arguments:
- tokens: bfloat16 [16, 8192, 1024], P('series', 'tm'), may hold values from -6 to 6
- gate_proj: bfloat16 [1024, 2048], replicated, may hold values from -0.1875 to 0.1875
- input_proj: bfloat16 [1024, 2304], replicated, may hold values from -0.1875 to 0.1875
- step_proj: bfloat16 [1024, 32], replicated, may hold values from -0.1875 to 0.1875
- conv_kernel: float32 [4, 2304], replicated, may hold values from -3 to 3
- conv_bias: float32 [2304], replicated, may hold values from -0.5 to 0.5
- step_bias: float32 [32], replicated, may hold values from -1 to 1
- decay_rate: float32 [32], replicated, may hold values from 6.1035156e-05 to 0.1
- skip_gain: float32 [32], replicated, may hold values from 0.5 to 1.5
- norm_gain: float32 [2048], replicated, may hold values from 0.1 to 1.9
- out_proj: bfloat16 [2048, 1024], replicated, may hold values from -0.125 to 0.125
- lengths: int32 [16], P('series'), may hold values from 256 to 8192, as said below
- slot_series: int32 [16], P('series'), may hold values from 0 to 15, each once
Outputs:
- mixed: bfloat16 [16, 8192, 1024], P('series', 'tm')
Inputs may be any that keep to these rules, and one draw needn't show every extreme that they name: `lengths`: multiples of 256; some series has the full 8192. `slot_series`: each series number appears once.
All inputs are finite; a program needn't handle non-finite values.
Results may differ from a plain program's by a relative error of at most 0.0054.
Values may be sent and summed in bfloat16 or wider, within the bound.
A program may use at most 128 MiB of HBM per device.

v0:
```python
import jax
import jax.numpy as jnp
from jax import lax
from jax.sharding import Mesh
from jax.sharding import PartitionSpec as P

DI = 2048
H = 32
P_SIZE = 64
N = 128
BLOCK = 256
TM = ("tm_0", "tm_1")


epsilon = 1e-05


def shifted(shard, axis, by):
    count = lax.axis_size(axis)
    pairs = [(i, i + by) for i in range(count) if 0 <= i + by < count]
    return lax.ppermute(shard, axis, pairs)


def from_everyone(shard, axis):
    copies = jnp.broadcast_to(shard, (lax.axis_size(axis), *shard.shape))
    return lax.all_to_all(copies, axis, split_axis=0, concat_axis=0, tiled=True)


def joined_along(pieces, dim):
    shape = list(pieces.shape[1:])
    shape[dim] *= pieces.shape[0]
    return jnp.moveaxis(pieces, 0, dim).reshape(shape)


def gather_directly(shard, axis, dim):
    pieces = from_everyone(shard, axis)
    return joined_along(pieces, dim)


def filled_with(shard, identity):
    return jax.tree.map(
        lambda a, e: jnp.broadcast_to(jnp.asarray(e, a.dtype), a.shape), shard, identity
    )


def entering(shard, axes, combine, identity):
    before = start = filled_with(shard, identity)
    total = shard
    for axis in reversed(axes):
        count, here = (lax.axis_size(axis), lax.axis_index(axis))
        pieces = jax.tree.map(lambda part: lax.all_gather(part, axis), total)
        inside, total = (start, start)
        for k in range(count):
            passed = k < here
            total = combine(total, jax.tree.map(lambda part: part[k], pieces))
            inside = jax.tree.map(lambda new, old: jnp.where(passed, new, old), total, inside)
        before = combine(inside, before)
    return before


def block_terms(inputs_x, inputs_b, inputs_c, step_sizes, decay_rate, skip_gain):
    width_q = inputs_x.shape[0]
    cumulative = jnp.cumsum(-step_sizes * decay_rate[None, :], axis=0)
    heads_cum = cumulative.T
    causal = jnp.tril(jnp.ones((width_q, width_q), dtype=bool))[None]
    segment = heads_cum[:, :, None] - heads_cum[:, None, :]
    decays = jnp.where(causal, jnp.exp(jnp.where(causal, segment, 0.0)), 0.0)
    scores = jnp.dot(inputs_c, inputs_b.T, preferred_element_type=jnp.float32)
    weights = (decays * scores[None] * step_sizes.T[:, None, :]).astype(jnp.bfloat16)
    intra = jnp.einsum("hts,shp->thp", weights, inputs_x, preferred_element_type=jnp.float32)
    partial_out = intra + skip_gain[None, :, None] * inputs_x.astype(jnp.float32)
    end_weight = jnp.exp(cumulative[-1][None, :] - cumulative) * step_sizes
    weighted_x = (inputs_x.astype(jnp.float32) * end_weight[:, :, None]).astype(jnp.bfloat16)
    increment = jnp.einsum("shp,sn->hpn", weighted_x, inputs_b, preferred_element_type=jnp.float32)
    return (partial_out, cumulative, increment)


def body(
    tokens,
    gate_proj,
    input_proj,
    step_proj,
    conv_kernel,
    conv_bias,
    step_bias,
    decay_rate,
    skip_gain,
    norm_gain,
    out_proj,
    lengths,
    slot_series,
):
    series_here, local_steps, model_width = tokens.shape
    flat_tokens = tokens.reshape(series_here * local_steps, model_width)
    gate = jnp.dot(flat_tokens, gate_proj, preferred_element_type=jnp.float32)
    mixed_raw = jnp.dot(flat_tokens, input_proj, preferred_element_type=jnp.float32).astype(
        jnp.bfloat16
    )
    mixed_raw = mixed_raw.reshape(series_here, local_steps, DI + 2 * N)
    step_raw = jnp.dot(flat_tokens, step_proj, preferred_element_type=jnp.float32).reshape(
        series_here, local_steps, H
    )
    kernel_len = conv_kernel.shape[0]
    rim_steps = mixed_raw[:, local_steps - (kernel_len - 1) :, :]
    earlier_rim = shifted(rim_steps, TM, 1)
    padded = jnp.concatenate([earlier_rim, mixed_raw], axis=1)
    convolved = jnp.zeros(mixed_raw.shape, jnp.float32) + conv_bias[None, None, :]
    for offset in range(kernel_len):
        convolved = convolved + conv_kernel[offset][None, None, :] * padded[
            :, offset : offset + local_steps
        ].astype(jnp.float32)
    activated = jax.nn.silu(convolved)
    all_lengths = gather_directly(lengths, "series", 0)
    matches = slot_series[:, None] == jnp.arange(all_lengths.shape[0], dtype=jnp.int32)[None, :]
    my_lengths = jnp.sum(jnp.where(matches, all_lengths[None, :], 0), axis=1)
    time_offset = lax.axis_index(TM) * local_steps
    positions = time_offset + jnp.arange(local_steps, dtype=jnp.int32)
    live = (positions[None, :] < my_lengths[:, None]).astype(jnp.float32)
    block_count = local_steps // BLOCK
    inputs_x = (
        activated[:, :, :DI]
        .astype(jnp.bfloat16)
        .reshape(series_here, block_count, BLOCK, H, P_SIZE)
    )
    inputs_b = (
        activated[:, :, DI : DI + N]
        .astype(jnp.bfloat16)
        .reshape(series_here, block_count, BLOCK, N)
    )
    inputs_c = (
        activated[:, :, DI + N :].astype(jnp.bfloat16).reshape(series_here, block_count, BLOCK, N)
    )
    step_sizes = (jax.nn.softplus(step_raw + step_bias[None, None, :]) * live[:, :, None]).reshape(
        series_here, block_count, BLOCK, H
    )
    block_starts = time_offset + jnp.arange(block_count, dtype=jnp.int32) * BLOCK
    block_live = block_starts[None, :] < my_lengths[:, None]

    def compute_terms(block_x, block_b, block_c, block_dt):
        return block_terms(block_x, block_b, block_c, block_dt, decay_rate, skip_gain)

    def series_pass(pieces):
        series_x, series_b, series_c, series_dt, series_live = pieces

        def advance(carried, block_pieces):
            block_x, block_b, block_c, block_dt, block_flag = block_pieces
            partial_out, cumulative, increment = compute_terms(block_x, block_b, block_c, block_dt)
            new_state = jnp.exp(cumulative[-1])[:, None, None] * carried + increment
            return (new_state, (partial_out, cumulative, carried))

        start_state = jnp.zeros((H, P_SIZE, N), jnp.float32)
        return lax.scan(
            advance, start_state, (series_x, series_b, series_c, series_dt, series_live)
        )

    end_states, (partials, cumulatives, befores) = lax.map(
        series_pass, (inputs_x, inputs_b, inputs_c, step_sizes, block_live)
    )
    block_decay = cumulatives[:, :, -1, :]
    device_decay = jnp.sum(block_decay, axis=1)

    def combine(before_part, after_part):
        return (
            before_part[0] + after_part[0],
            jnp.exp(after_part[0])[:, :, None, None] * before_part[1] + after_part[1],
        )

    prefix_parts = entering(
        (device_decay, end_states),
        TM,
        combine,
        (jnp.zeros_like(device_decay), jnp.zeros_like(end_states)),
    )
    incoming = prefix_parts[1]
    before_decay = jnp.cumsum(block_decay, axis=1) - block_decay
    states_in = jnp.exp(before_decay)[:, :, :, None, None] * incoming[:, None] + befores
    states_bf = states_in.astype(jnp.bfloat16)
    inter = jnp.einsum("sctn,schpn->scthp", inputs_c, states_bf, preferred_element_type=jnp.float32)
    outputs = partials + jnp.exp(cumulatives)[:, :, :, :, None] * inter
    outputs = outputs.reshape(series_here * local_steps, DI)
    gated = outputs * jax.nn.silu(gate)
    scale = lax.rsqrt(jnp.mean(gated * gated, axis=1, keepdims=True) + epsilon)
    normed = (gated * scale * norm_gain[None, :]).astype(jnp.bfloat16)
    result = jnp.dot(normed, out_proj, preferred_element_type=jnp.float32).reshape(
        series_here, local_steps, model_width
    )
    return (result * live[:, :, None]).astype(jnp.bfloat16)


def solution(mesh):
    split = Mesh(mesh.devices.reshape(4, 4, mesh.shape["series"]), ("tm_0", "tm_1", "series"))
    in_specs = (
        P("series", TM, None),
        P(),
        P(),
        P(),
        P(),
        P(),
        P(),
        P(),
        P(),
        P(),
        P(),
        P("series"),
        P("series"),
    )
    out_specs = P("series", TM, None)
    return jax.shard_map(body, mesh=split, in_specs=in_specs, out_specs=out_specs, check_vma=False)
```

profile of v0, /device:TPU:1, one launch (start us, length us, event | category | flops | bytes accessed | tf_op | source)
XLA Modules:
  0.0 387.2 jit_solution(4595389706721508244)
XLA Ops:
  6.5 1.6 copy-done
  8.1 7.6 %convolution_convert_fusion = bf16[1024,2304]{1,0:T(8,128)(2,1)S(1)} fusion(bf16[1024,1024]{1,0:T(8,128)(2,1)S(1)} %bitcast.232, bf16[1024,2304]{1,0:T(8,128)(2,1)} %param.19), kind=kOutput, calls=%fused_computation.61 | convolution fusion | flops 4834197504 | bytes 11534336 | tf_op jit(solution)/shard_map/dot_general | solution.py:96
  15.7 2.1 copy-done.3
  17.9 4.0 %collective-permute-start = (bf16[2,3,2304]{2,0,1:T(2,128)(2,1)S(1)}, bf16[2,3,2304]{2,0,1:T(2,128)(2,1)S(1)}, u32[]{:S(2)}, u32[]{:S(2)}) collective-permute-start(bf16[2,3,2304]{2,0,1:T(2,128)(2,1)S(1)} %copy.72), channel_id=1, source_target_pairs={{0,8},{8,16},{16,24},{24,32},{32,40},{40,48},{48,56},{56,64},{64,7... | collective-permute-start | bytes 82952 | tf_op jit(solution)/shard_map/ppermute | solution.py:21
  22.5 6.3 %all-to-all-start = ((s32[8,1,2]{2,1,0:T(1,128)}), s32[8,1,2]{2,1,0:T(1,128)S(1)}, u32[]{:S(2)}, u32[]{:S(2)}) async-start(s32[8,1,2]{2,1,0:T(1,128)} %broadcast_in_dim.110), calls=%async_computation | async-start | bytes 8192 | tf_op jit(solution)/shard_map/all_to_all | solution.py:26
  28.9 6.7 %copy.59 = bf16[2,512,2304]{1,2,0:T(8,128)(2,1)} copy(bf16[2,512,2304]{2,1,0:T(8,128)(2,1)} %bitcast.239) | data formatting | bytes 9437184 | tf_op jit(solution)/shard_map/reshape | solution.py:99
  39.5 14.4 %multiply_convert_fusion.5 = bf16[2,512,2304]{1,2,0:T(8,128)(2,1)S(1)} fusion(bf16[2,512,2304]{1,2,0:T(8,128)(2,1)} %copy.59, bf16[2,3,2304]{1,2,0:T(8,128)(2,1)S(1)} %copy.58, f32[2304]{0:T(1024)S(1)} %get-tuple-element.224, f32[2304]{0:T(1024)S(1)} %get-tuple-element.225, f32[2304]{0:T(1024)S(1)} %get-tuple-element.223, f32[2304]{0:T(1024)S(1)} %get-tuple-element.222, ...), kind=kLoop, calls=%fused_computation.52 | loop fusion | flops 61341696 | bytes 9510912 | tf_op jit(solution)/shard_map/convert.2
  54.1 2.2 slice.147
  58.0 6.9 %reshape.294 = bf16[2,2,256,32,64]{2,1,4,3,0:T(2,128)(2,1)} reshape(bf16[2,512,2048]{1,2,0:T(8,128)(2,1)} %slice.147) | data formatting | bytes 8388608 | tf_op jit(solution)/shard_map/reshape | solution.py:123
  64.9 75.8 %while.37 = (s32[]{:T(128)}, f32[2,32,64,128]{3,2,1,0:T(8,128)}, f32[2,2,256,32,64]{2,4,3,1,0:T(8,128)}, f32[2,2,256,32]{2,3,1,0:T(8,128)}, f32[2,2,32,64,128]{4...) while((s32[]{:T(128)}, f32[2,32,64,128]{3,2,1,0:T(8,128)}, ...), condition=%wide.region_6.7_spmd.clone, body=%wide.region_1.6_spmd.sunk.clone | while | flops 437370976 | bytes 94643856 | solution.py:156
  65.9 3.3 constant_dynamic-slice_fusion.7
  69.2 1.8 copy.100
  71.8 20.8 %while.36 = (s32[]{:T(128)}, f32[32,64,128]{2,1,0:T(8,128)S(1)}, f32[2,256,32,64]{1,3,2,0:T(8,128)}, f32[2,256,32]{1,2,0:T(8,128)}, f32[2,32,64,128]{3,2,1,0:T(8...) while((s32[]{:T(128)}, f32[32,64,128]{2,1,0:T(8,128)S(1)}, ...), condition=%wide.region_5.5_spmd.clone, body=%wide.region_2.4_spmd.clone.sunk | while | flops 437370976 | bytes 10887844 | solution.py:152
  73.0 5.5 %bitcast_dynamic-update-slice_fusion.18 = f32[2,256,32,64]{1,3,2,0:T(8,128)} fusion(f32[2,256,32,64]{1,3,2,0:T(8,128)} %get-tuple-element.518, s32[]{:T(128)} %get-tuple-element.516, f32[32,256]{1,0:T(8,128)S(1)} %dynamic-slice_bitcast_fusion.6, f32[256,256]{1,0:T(8,128)S(1)} %fusion.76, f32[32,256]{1,0:T(8,128)S(1)} %get-tuple-element.460, ...), kind=kOutput, calls=%fused_computation.8.clone.1 | convolution fusion | flops 282591232 | bytes 4621824 | tf_op jit(solution)/shard_map/while/body/eval_jaxpr/while/body/eval_jaxpr/hts,shp->thp/dot_general | solution.py:70
  78.8 1.1 bitcast_dynamic-update-slice_fusion.20
  79.9 1.8 convolution_add_fusion.3
  83.5 5.4 %bitcast_dynamic-update-slice_fusion.18 = f32[2,256,32,64]{1,3,2,0:T(8,128)} fusion(f32[2,256,32,64]{1,3,2,0:T(8,128)} %get-tuple-element.518, s32[]{:T(128)} %get-tuple-element.516, f32[32,256]{1,0:T(8,128)S(1)} %dynamic-slice_bitcast_fusion.6, f32[256,256]{1,0:T(8,128)S(1)} %fusion.76, f32[32,256]{1,0:T(8,128)S(1)} %get-tuple-element.460, ...), kind=kOutput, calls=%fused_computation.8.clone.1 | convolution fusion | flops 282591232 | bytes 4621824 | tf_op jit(solution)/shard_map/while/body/eval_jaxpr/while/body/eval_jaxpr/hts,shp->thp/dot_general | solution.py:70
  89.2 1.1 bitcast_dynamic-update-slice_fusion.20
  90.2 1.8 convolution_add_fusion.3
  92.7 4.8 %bitcast_dynamic-update-slice_fusion.22 = f32[2,2,256,32,64]{2,4,3,1,0:T(8,128)} fusion(f32[2,2,256,32,64]{2,4,3,1,0:T(8,128)} %get-tuple-element.560, s32[]{:T(128)} %get-tuple-element.558, f32[2,256,32,64]{1,3,2,0:T(8,128)} %get-tuple-element.478), kind=kLoop, calls=%fused_computation.42.clone.1.clone | loop fusion | bytes 8389120 | tf_op jit(solution)/shard_map/while/body/jit(dynamic_update_index_in_dim)/dynamic_update_slice | solution.py:156
  97.7 2.1 copy-done.7
  100.0 1.3 copy-done.8
  103.8 3.3 constant_dynamic-slice_fusion.7
  107.1 1.8 copy.100
  109.7 20.8 %while.36 = (s32[]{:T(128)}, f32[32,64,128]{2,1,0:T(8,128)S(1)}, f32[2,256,32,64]{1,3,2,0:T(8,128)}, f32[2,256,32]{1,2,0:T(8,128)}, f32[2,32,64,128]{3,2,1,0:T(8...) while((s32[]{:T(128)}, f32[32,64,128]{2,1,0:T(8,128)S(1)}, ...), condition=%wide.region_5.5_spmd.clone, body=%wide.region_2.4_spmd.clone.sunk | while | flops 437370976 | bytes 10887844 | solution.py:152
  110.9 5.5 %bitcast_dynamic-update-slice_fusion.18 = f32[2,256,32,64]{1,3,2,0:T(8,128)} fusion(f32[2,256,32,64]{1,3,2,0:T(8,128)} %get-tuple-element.518, s32[]{:T(128)} %get-tuple-element.516, f32[32,256]{1,0:T(8,128)S(1)} %dynamic-slice_bitcast_fusion.6, f32[256,256]{1,0:T(8,128)S(1)} %fusion.76, f32[32,256]{1,0:T(8,128)S(1)} %get-tuple-element.460, ...), kind=kOutput, calls=%fused_computation.8.clone.1 | convolution fusion | flops 282591232 | bytes 4621824 | tf_op jit(solution)/shard_map/while/body/eval_jaxpr/while/body/eval_jaxpr/hts,shp->thp/dot_general | solution.py:70
  116.7 1.1 bitcast_dynamic-update-slice_fusion.20
  117.7 1.8 convolution_add_fusion.3
  121.4 5.4 %bitcast_dynamic-update-slice_fusion.18 = f32[2,256,32,64]{1,3,2,0:T(8,128)} fusion(f32[2,256,32,64]{1,3,2,0:T(8,128)} %get-tuple-element.518, s32[]{:T(128)} %get-tuple-element.516, f32[32,256]{1,0:T(8,128)S(1)} %dynamic-slice_bitcast_fusion.6, f32[256,256]{1,0:T(8,128)S(1)} %fusion.76, f32[32,256]{1,0:T(8,128)S(1)} %get-tuple-element.460, ...), kind=kOutput, calls=%fused_computation.8.clone.1 | convolution fusion | flops 282591232 | bytes 4621824 | tf_op jit(solution)/shard_map/while/body/eval_jaxpr/while/body/eval_jaxpr/hts,shp->thp/dot_general | solution.py:70
  127.0 1.1 bitcast_dynamic-update-slice_fusion.20
  128.1 1.8 convolution_add_fusion.3
  130.5 4.8 %bitcast_dynamic-update-slice_fusion.22 = f32[2,2,256,32,64]{2,4,3,1,0:T(8,128)} fusion(f32[2,2,256,32,64]{2,4,3,1,0:T(8,128)} %get-tuple-element.560, s32[]{:T(128)} %get-tuple-element.558, f32[2,256,32,64]{1,3,2,0:T(8,128)} %get-tuple-element.478), kind=kLoop, calls=%fused_computation.42.clone.1.clone | loop fusion | bytes 8389120 | tf_op jit(solution)/shard_map/while/body/jit(dynamic_update_index_in_dim)/dynamic_update_slice | solution.py:156
  135.6 2.1 copy-done.7
  137.9 1.3 copy-done.8
  140.8 1.0 slice_reduce_fusion.3
  141.8 7.7 %all-gather.2 = f32[4,2,32]{2,1,0:T(2,128)S(1)} all-gather(f32[1,2,32]{2,1,0:T(2,128)S(1)} %bitcast.241), channel_id=2, replica_groups=mesh['tm_0'=4,'tm_1'=4,'series'=8] {'tm_1'}, dimensions={0}, use_global_device_ids=true | all-gather | bytes 1280 | tf_op jit(solution)/shard_map/all_gather | solution.py:51
  149.5 75.2 %all-gather.8.cloned.1.call-done = f32[8,32,64,128]{3,2,1,0:T(8,128)} async-done(((f32[2,32,64,128]{3,2,1,0:T(8,128)}), f32[8,32,64,128]{3,2,1,0:T(8,128)}) %all-gather.8.cloned.1.call-update) | async-done | bytes 8388624 | tf_op jit(solution)/shard_map/all_gather | solution.py:51
  224.7 4.8 %bitcast_add_fusion.1 = f32[1,2,32,64,128]{4,3,2,1,0:T(8,128)} fusion(f32[8,32,64,128]{3,2,1,0:T(8,128)} %all-gather.8.cloned.1.call-done, f32[2,32]{1,0:T(2,128)S(1)} %get-tuple-element.281, f32[2,32]{1,0:T(2,128)S(1)} %get-tuple-element.280, f32[2,32]{1,0:T(2,128)S(1)} %get-tuple-element.278, f32[2,32]{1,0:T(2,128)S(1)} %get-tuple-element.279), kind=kLoop, calls=%fused_computation.81 | loop fusion | flops 3670016 | bytes 10486784 | tf_op jit(solution)/shard_map/add | solution.py:165
  229.6 7.6 %all_gather.22 = f32[4,2,32]{2,1,0:T(2,128)S(1)} all-gather(f32[1,2,32]{2,1,0:T(2,128)S(1)} %get-tuple-element.277), channel_id=1, replica_groups=mesh['tm_0'=4,'tm_1'=4,'series'=8] {'tm_0'}, dimensions={0}, use_global_device_ids=true | all-gather | bytes 1280 | tf_op jit(solution)/shard_map/all_gather | solution.py:51
  237.2 76.4 %all-gather.6.cloned.1.call-done = f32[4,2,32,64,128]{4,3,2,1,0:T(8,128)} async-done(((f32[1,2,32,64,128]{4,3,2,1,0:T(8,128)}), f32[4,2,32,64,128]{4,3,2,1,0:T(8,128)}) %all-gather.6.cloned.1.call-update) | async-done | bytes 8388624 | tf_op jit(solution)/shard_map/all_gather | solution.py:51
  313.6 8.0 %fusion.35 = f32[2,32,64,128]{3,2,1,0:T(8,128)S(1)} fusion(f32[4,2,32,64,128]{4,3,2,1,0:T(8,128)} %all-gather.6.cloned.1.call-done, f32[8,32,64,128]{3,2,1,0:T(8,128)} %all-gather.8.cloned.1.call-done, f32[2,32]{1,0:T(2,128)S(1)} %get-tuple-element.280, f32[2,32]{1,0:T(2,128)S(1)} %get-tuple-element.279, f32[2,32]{1,0:T(2,128)S(1)} %get-tuple-element.278, ...), kind=kLoop, calls=%fused_computation.74 | loop fusion | flops 12582912 | bytes 18876680 | tf_op jit(solution)/shard_map/add | solution.py:165
  321.9 1.2 copy-done.6
  323.1 5.0 %multiply_add_fusion = f32[2,2,256,32,64]{2,4,3,1,0:T(8,128)} fusion(f32[2,2,256,32,64]{2,4,3,1,0:T(8,128)S(1)} %bitcast.237, f32[2,2,256,32]{2,3,1,0:T(8,128)S(1)} %exp.120, bf16[2,2,256,128,1]{3,2,4,1,0:T(8,128)(2,1)} %bitcast.14, f32[2,2,32,64,128]{4,3,2,1,0:T(8,128)S(1)} %copy-done.6, f32[2,32,64,128]{3,2,1,0:T(8,128)S(1)} %fusion.35, ...), kind=kOutput, calls=%fused_computation.56 | convolution fusion | flops 544210944 | bytes 23462400 | tf_op jit(solution)/shard_map/sctn,schpn->scthp/dot_general | solution.py:178
  328.1 16.2 %copy.68 = f32[2,2,256,32,64]{4,3,2,1,0:T(8,128)} copy(f32[2,2,256,32,64]{2,4,3,1,0:T(8,128)} %multiply_add_fusion) | data formatting | bytes 16777216 | tf_op jit(solution)/shard_map/reshape | solution.py:180
  344.3 14.9 %reshape.364 = f32[1024,2048]{1,0:T(8,128)} reshape(f32[2,2,256,32,64]{4,3,2,1,0:T(8,128)} %copy.68) | data formatting | bytes 16777216 | tf_op jit(solution)/shard_map/reshape | solution.py:180
  359.2 11.5 %multiply_reduce_fusion = (f32[1024]{0:T(1024)S(1)}, f32[1024,2048]{1,0:T(8,128)}) fusion(f32[1024,2048]{1,0:T(8,128)} %reshape.364, bf16[1024,1024]{1,0:T(8,128)(2,1)S(1)} %bitcast.233, bf16[1024,2048]{1,0:T(8,128)(2,1)} %param.18), kind=kOutput, calls=%fused_computation.54 | convolution fusion | flops 4309646336 | bytes 23072768 | tf_op jit(solution)/shard_map/dot_general | solution.py:95
  370.7 8.0 %fusion.29 = f32[1024,1024]{1,0:T(8,128)S(1)} fusion(bf16[2048,1024]{1,0:T(8,128)(2,1)S(1)} %copy-done.20, f32[2048]{0:T(1024)S(1)} %copy-done.21, f32[1024]{0:T(1024)S(1)} %add_rsqrt_fusion, f32[1024,2048]{1,0:T(8,128)S(1)} %copy-done.2, f32[1024,2048]{1,0:T(8,128)} %get-tuple-element.287), kind=kOutput, calls=%fused_computation.65 | convolution fusion | flops 4311744512 | bytes 25178112 | tf_op jit(solution)/shard_map/dot_general | solution.py:184
  378.8 1.6 multiply_convert_fusion.8
  (164 shorter events, 22.7 us)
Async XLA Ops:
  6.5 1.6 copy-start
  8.1 13.8 %copy-start.19 = (s32[2]{0:T(128)S(1)}, s32[2]{0:T(128)}, u32[]{:S(2)}) copy-start(s32[2]{0:T(128)} %param.28) | copy-start | bytes 28
  15.7 2.1 copy-start.3
  17.9 20.9 %collective-permute-start = (bf16[2,3,2304]{2,0,1:T(2,128)(2,1)S(1)}, bf16[2,3,2304]{2,0,1:T(2,128)(2,1)S(1)}, u32[]{:S(2)}, u32[]{:S(2)}) collective-permute-start(bf16[2,3,2304]{2,0,1:T(2,128)(2,1)S(1)} %copy.72), channel_id=1, source_target_pairs={{0,8},{8,16},{16,24},{24,32},{32,40},{40,48},{48,56},{56,64},{64,7... | collective-permute-start | bytes 82952 | tf_op jit(solution)/shard_map/ppermute | solution.py:21
  22.5 13.2 %all-to-all-start = ((s32[8,1,2]{2,1,0:T(1,128)}), s32[8,1,2]{2,1,0:T(1,128)S(1)}, u32[]{:S(2)}, u32[]{:S(2)}) async-start(s32[8,1,2]{2,1,0:T(1,128)} %broadcast_in_dim.110), calls=%async_computation | async-start | bytes 8192 | tf_op jit(solution)/shard_map/all_to_all | solution.py:26
  28.8 6.8 %copy-start.14 = (f32[4,2304]{1,0:T(4,128)S(1)}, f32[4,2304]{1,0:T(4,128)}, u32[]{:S(2)}) copy-start(f32[4,2304]{1,0:T(4,128)} %param.21) | copy-start | bytes 110596
  28.8 8.3 %copy-start.22 = (s32[2]{0:T(128)S(1)}, s32[2]{0:T(128)}, u32[]{:S(2)}) copy-start(s32[2]{0:T(128)} %param.29) | copy-start | bytes 28
  28.8 8.5 %copy-start.13 = (bf16[1024,32]{0,1:T(8,128)(2,1)S(1)}, bf16[1024,32]{0,1:T(8,128)(2,1)}, u32[]{:S(2)}) copy-start(bf16[1024,32]{0,1:T(8,128)(2,1)} %param.20) | copy-start | bytes 196612
  28.8 8.5 %copy-start.18 = (f32[32]{0:T(128)S(1)}, f32[32]{0:T(128)}, u32[]{:S(2)}) copy-start(f32[32]{0:T(128)} %param.23) | copy-start | bytes 388
  28.8 10.7 %copy-start.17 = (f32[2304]{0:T(1024)S(1)}, f32[2304]{0:T(1024)}, u32[]{:S(2)}) copy-start(f32[2304]{0:T(1024)} %param.22) | copy-start | bytes 27652
  28.8 195.9 %all-gather.8.cloned.1.call-start = ((), (), s32[]{:S(2)}) async-start(), calls=%async_computation.2 | async-start | bytes 10485760 | tf_op jit(solution)/shard_map/all_gather | solution.py:51
  37.3 1.5 copy-start.15
  57.9 6.9 %copy-start.9 = (f32[32]{0:T(128)S(1)}, f32[32]{0:T(128)}, u32[]{:S(2)}) copy-start(f32[32]{0:T(128)} %param.24) | copy-start | bytes 388
  57.9 6.9 %copy-start.23 = (f32[32]{0:T(128)S(1)}, f32[32]{0:T(128)}, u32[]{:S(2)}) copy-start(f32[32]{0:T(128)} %param.25) | copy-start | bytes 388
  92.7 4.8 %copy-start.1 = (f32[2,32,64,128]{3,2,1,0:T(8,128)S(1)}, f32[2,32,64,128]{3,2,1,0:T(8,128)}, u32[]{:S(2)}) copy-start(f32[2,32,64,128]{3,2,1,0:T(8,128)} %get-tuple-element.480) | copy-start | bytes 6291460 | tf_op jit(solution)/shard_map/while
  92.7 4.8 %copy-start.4 = (f32[2,2,32,64,128]{4,3,2,1,0:T(8,128)S(1)}, f32[2,2,32,64,128]{4,3,2,1,0:T(8,128)}, u32[]{:S(2)}) copy-start(f32[2,2,32,64,128]{4,3,2,1,0:T(8,128)} %get-tuple-element.562) | copy-start | bytes 12582916 | tf_op jit(solution)/shard_map/while
  97.4 2.4 copy-start.7
  97.4 3.9 copy-start.10
  97.7 2.2 copy-start.5
  100.0 1.3 copy-start.8
  102.1 0.6 copy-start.11
  130.5 4.8 %copy-start.1 = (f32[2,32,64,128]{3,2,1,0:T(8,128)S(1)}, f32[2,32,64,128]{3,2,1,0:T(8,128)}, u32[]{:S(2)}) copy-start(f32[2,32,64,128]{3,2,1,0:T(8,128)} %get-tuple-element.480) | copy-start | bytes 6291460 | tf_op jit(solution)/shard_map/while
  130.5 4.8 %copy-start.4 = (f32[2,2,32,64,128]{4,3,2,1,0:T(8,128)S(1)}, f32[2,2,32,64,128]{4,3,2,1,0:T(8,128)}, u32[]{:S(2)}) copy-start(f32[2,2,32,64,128]{4,3,2,1,0:T(8,128)} %get-tuple-element.562) | copy-start | bytes 12582916 | tf_op jit(solution)/shard_map/while
  135.3 2.4 copy-start.7
  135.3 3.9 copy-start.10
  135.6 2.2 copy-start.5
  137.9 1.3 copy-start.8
  140.0 0.6 copy-start.11
  140.7 172.9 %all-gather.6.cloned.1.call-start = ((), (), s32[]{:S(2)}) async-start(), calls=%async_computation.1 | async-start | bytes 10485760 | tf_op jit(solution)/shard_map/all_gather | solution.py:51
  224.7 4.8 %copy-start.12 = (f32[2,2,256,32]{2,3,1,0:T(8,128)S(1)}, f32[2,2,256,32]{2,3,1,0:T(8,128)}, u32[]{:S(2)}) copy-start(f32[2,2,256,32]{2,3,1,0:T(8,128)} %get-tuple-element.616) | copy-start | bytes 393220
  313.6 8.0 %slice-start = ((s8[8388608]{0:T(1024)(128)(4,1)}), s8[4194304]{0:T(1024)(128)(4,1)S(1)}, s32[]{:S(2)}) async-start(s8[8388608]{0:T(1024)(128)(4,1)} %bitcast.236), calls=%async_computation.3 | async-start | bytes 8388608
  313.6 8.3 %slice-start.1 = ((s8[8388608]{0:T(1024)(128)(4,1)}), s8[4194304]{0:T(1024)(128)(4,1)S(1)}, s32[]{:S(2)}) async-start(s8[8388608]{0:T(1024)(128)(4,1)} %bitcast.236), calls=%async_computation.4 | async-start | bytes 8388608
  313.6 9.5 %copy-start.6 = (f32[2,2,32,64,128]{4,3,2,1,0:T(8,128)S(1)}, f32[2,2,32,64,128]{4,3,2,1,0:T(8,128)}, u32[]{:S(2)}) copy-start(f32[2,2,32,64,128]{4,3,2,1,0:T(8,128)} %get-tuple-element.617) | copy-start | bytes 12582916
  359.2 11.5 %copy-start.2 = (f32[1024,2048]{1,0:T(8,128)S(1)}, f32[1024,2048]{1,0:T(8,128)}, u32[]{:S(2)}) copy-start(f32[1024,2048]{1,0:T(8,128)} %reshape.364) | copy-start | bytes 25165828
  359.2 11.5 %copy-start.20 = (bf16[2048,1024]{1,0:T(8,128)(2,1)S(1)}, bf16[2048,1024]{1,0:T(8,128)(2,1)}, u32[]{:S(2)}) copy-start(bf16[2048,1024]{1,0:T(8,128)(2,1)} %param.27) | copy-start | bytes 12582916
  359.2 11.5 %copy-start.21 = (f32[2048]{0:T(1024)S(1)}, f32[2048]{0:T(1024)}, u32[]{:S(2)}) copy-start(f32[2048]{0:T(1024)} %param.26) | copy-start | bytes 24580
  370.7 8.0 %copy-start.16 = (f32[2,512]{1,0:T(2,128)S(1)}, f32[2,512]{1,0:T(2,128)}, u32[]{:S(2)}) copy-start(f32[2,512]{1,0:T(2,128)} %copy-done.15) | copy-start | bytes 12292
Sparse Core Ops, SparseCore 0:
  140.8 83.8 all-gather.7
  229.6 83.9 all-gather.5
where the time goes:
time: 389 us; the launch traced here: 387 us
  waiting for transfers between devices  152 us (39%)
  local copies, waits for them, and re-layouts  92.1 us (24%)
  matrix products  62.3 us (16%)
  other arithmetic  41.4 us (11%)
  blocking collectives  15.4 us (4%)
  between operations  13.7 us (4%)
  starting transfers between devices  10.4 us (3%)
    all_gather x2, waiting for transfers between devices, entering(): pieces = jax.tree.map(lambda part: lax.all_gather(part, axis), total)  152 us
    reshape x2, local copies, waits for them, and re-layouts, body(): outputs = outputs.reshape(series_here * local_steps, DI)  31.1 us
    dot_general x4, matrix products, block_terms(): jnp.einsum('hts,shp->thp', weights, inputs_x, preferred_element_type=jnp....  21.6 us
    another operation x20, other arithmetic  17.2 us
    all_gather x2, blocking collectives, entering(): pieces = jax.tree.map(lambda part: lax.all_gather(part, axis), total)  15.4 us
    add x2, other arithmetic, combine(): jnp.exp(after_part[0])[:, :, None, None] * before_part[1] + after_part[1]  12.8 us
    dynamic_update_slice x8, local copies, waits for them, and re-layouts, body(): lax.map(series_pass, (inputs_x, inputs_b, inputs_c, step_sizes, block_live))  12 us
    dynamic_slice x8, local copies, waits for them, and re-layouts, body(): lax.map(series_pass, (inputs_x, inputs_b, inputs_c, step_sizes, block_live))  11.8 us
  transfers between devices with their start and end apart: 4, of which 2 were waited for; matrix products, arithmetic and copies ran while one was open for 3% of the time, Pallas kernels for 0%

commit v1 on v0

v1 whole, which is shorter than its diff:
```python
import functools

import jax
import jax.numpy as jnp
from jax import lax
from jax.experimental import pallas as pl
from jax.experimental.pallas import tpu as pltpu
from jax.sharding import PartitionSpec as P

MESH = pl.DeviceIdType.MESH
F32 = jnp.float32
BF16 = jnp.bfloat16

D = 1024
DI = 2048
H = 32
N = 128
KT = 4
W_IN = DI + 2 * N
Q = 128
EPS = 1e-05
LOG2E = 1.4426950408889634
RIM = 16
GROUPS = 4
GC = DI // GROUPS


def dot(a, b, **kw):
    return jnp.dot(a, b, preferred_element_type=F32, **kw)


def hilo(v):
    hi = v.astype(BF16)
    lo = (v - hi.astype(F32)).astype(BF16)
    return jnp.concatenate([hi, lo], axis=1)


def kernel(
    n_tm,
    n_ser,
    series_here,
    steps,
    tokens_hbm,
    gate_hbm,
    in_hbm,
    stepw_ref,
    convk_ref,
    convb_ref,
    stepb_ref,
    rate_ref,
    skip_ref,
    gain_ref,
    out_w_hbm,
    len_smem,
    slot_smem,
    out_hbm,
    tok,
    win,
    wgate,
    wout,
    xs,
    bt,
    raw,
    cumc,
    crt,
    fhl,
    ghl,
    eh,
    rows,
    rowx,
    sl,
    scur,
    sin,
    yb,
    sg,
    nb,
    isend,
    irecv,
    ssend,
    srecv,
    dsend,
    drecv,
    dxs,
    lsend,
    lrecv,
    lenv,
    load_sem,
    out_sem,
    len_ssem,
    len_rsem,
    rim_ssem,
    rim_rsem,
    d_ssem,
    d_rsem,
    i_ssem,
    i_rsem,
    s_ssem,
    s_rsem,
):
    me = lax.axis_index("tm")
    ser = lax.axis_index("series")
    chunks = steps // Q
    nc = series_here * chunks

    loads = []
    for s in range(series_here):
        loads.append(
            pltpu.make_async_copy(
                tokens_hbm.at[s], tok.at[s, pl.ds(RIM, steps), :], load_sem.at[s]
            )
        )
    loads.append(pltpu.make_async_copy(in_hbm, win, load_sem.at[2]))
    loads.append(pltpu.make_async_copy(gate_hbm, wgate, load_sem.at[3]))
    loads.append(pltpu.make_async_copy(out_w_hbm, wout, load_sem.at[4]))
    for c in loads:
        c.start()

    barrier = pltpu.get_barrier_semaphore()

    def greet_tm(k, carry):
        @pl.when(k != me)
        def _():
            pl.semaphore_signal(barrier, inc=1, device_id=(k, ser), device_id_type=MESH)

        return carry

    def greet_ser(k, carry):
        @pl.when(k != ser)
        def _():
            pl.semaphore_signal(barrier, inc=1, device_id=(me, k), device_id_type=MESH)

        return carry

    lax.fori_loop(0, n_tm, greet_tm, 0)
    lax.fori_loop(0, n_ser, greet_ser, 0)

    lane = lax.broadcasted_iota(jnp.int32, (8, 128), 1)
    lsend[...] = jnp.where(lane == 0, len_smem[0], jnp.where(lane == 1, len_smem[1], 0))
    er = lax.broadcasted_iota(jnp.int32, (2 * H, DI), 0)
    ec = lax.broadcasted_iota(jnp.int32, (2 * H, DI), 1)
    eh[...] = jnp.where((er % H) == ec // (DI // H), 1.0, 0.0).astype(BF16)
    dsend[...] = jnp.zeros_like(dsend)
    rows[...] = jnp.zeros_like(rows)

    pl.semaphore_wait(barrier, n_tm + n_ser - 2)

    def len_copy(k, slot):
        return pltpu.make_async_remote_copy(
            src_ref=lsend,
            dst_ref=lrecv.at[slot],
            send_sem=len_ssem.at[k],
            recv_sem=len_rsem.at[slot],
            device_id=(me, k),
            device_id_type=MESH,
        )

    def send_len(k, carry):
        @pl.when(k != ser)
        def _():
            len_copy(k, ser).start()

        return carry

    lax.fori_loop(0, n_ser, send_len, 0)
    lrecv[ser] = lsend[...]

    def rim_copy(s):
        return pltpu.make_async_remote_copy(
            src_ref=tokens_hbm.at[s, pl.ds(steps - RIM, RIM), :],
            dst_ref=tok.at[s, pl.ds(0, RIM), :],
            send_sem=rim_ssem.at[s],
            recv_sem=rim_rsem.at[s],
            device_id=(lax.rem(me + 1, n_tm), ser),
            device_id_type=MESH,
        )

    @pl.when(me < n_tm - 1)
    def _():
        for s in range(series_here):
            rim_copy(s).start()

    @pl.when(me == 0)
    def _():
        for s in range(series_here):
            tok[s, 0:RIM, :] = jnp.zeros((RIM, D), BF16)

    def wait_len(k, carry):
        @pl.when(k != ser)
        def _():
            len_copy(k, k).wait_recv()

        return carry

    lax.fori_loop(0, n_ser, wait_len, 0)
    for s in range(series_here):
        sid = slot_smem[s]
        found = jnp.zeros((8, 128), jnp.int32)
        for p in range(n_ser):
            hit = (lane < series_here) & (lane + series_here * p == sid)
            found = found + jnp.where(hit, lrecv[p], 0)
        lenv[s] = jnp.broadcast_to(
            jnp.sum(found.astype(F32), axis=1, keepdims=True), (8, 128)
        )

    for s in range(series_here):
        loads[s].wait()

    tri_r = lax.broadcasted_iota(jnp.int32, (Q, Q), 0)
    tri_c = lax.broadcasted_iota(jnp.int32, (Q, Q), 1)
    neg_rate = rate_ref[...].reshape(1, H) * (-LOG2E)
    step_bias = stepb_ref[...].reshape(1, H)

    def steps_body(ci, carry):
        s = ci // chunks
        c = ci % chunks
        t0 = pl.multiple_of(RIM + c * Q, 16)
        pre = dot(tok[s, pl.ds(t0, Q), :], stepw_ref[...]) + step_bias
        first = (me * steps + c * Q).astype(F32)
        live = jnp.where(lenv[s] > first, 1.0, 0.0)
        dt = jnp.maximum(pre, 0.0) + jnp.log1p(jnp.exp(-jnp.abs(pre)))
        dt = dt * live[0:1, 0:H]
        ltri = jnp.where(tri_r >= tri_c, 1.0, 0.0)
        cum = dot(ltri, dt * neg_rate, precision=lax.Precision.HIGHEST)
        lg = jnp.where(dt > 0.0, jnp.log(jnp.where(dt > 0.0, dt, 1.0)) * LOG2E, -1e30)
        crp = cum - lg
        last = cum[Q - 1 : Q, :]
        cumc[ci] = cum
        fhl[ci] = hilo(jnp.exp2(last - crp))
        ghl[ci] = hilo(jnp.exp2(cum))
        wide = jnp.concatenate([crp, jnp.zeros((Q, 128 - H), F32)], axis=1)
        crt[ci] = wide.T[0:H, :]
        return carry

    lax.fori_loop(0, nc, steps_body, 0)

    r8 = lax.broadcasted_iota(jnp.int32, (8, H), 0)
    ecl = jnp.zeros((8, H), F32)
    ebef = jnp.zeros((8, H), F32)
    dtot = jnp.zeros((8, H), F32)
    for s in range(series_here):
        before = jnp.zeros((1, H), F32)
        for c in range(chunks):
            ci = s * chunks + c
            last = cumc[ci, Q - 1 : Q, :]
            ecl = jnp.where(r8 == ci, jnp.exp2(last), ecl)
            ebef = jnp.where(r8 == ci, jnp.exp2(before), ebef)
            before = before + last
        dtot = jnp.where(r8 == s, before, dtot)
    dsend[:, 0:H] = dtot
    rows[0:8, :] = ecl
    rows[8:16, :] = ebef
    rows[16:24, :] = jnp.broadcast_to(skip_ref[...].reshape(1, H), (8, H))
    rowx[...] = dot(hilo(rows[...]), eh[...])

    def d_copy(k, slot):
        return pltpu.make_async_remote_copy(
            src_ref=dsend,
            dst_ref=drecv.at[slot],
            send_sem=d_ssem.at[k],
            recv_sem=d_rsem.at[slot],
            device_id=(k, ser),
            device_id_type=MESH,
        )

    def send_d(k, carry):
        @pl.when(k != me)
        def _():
            d_copy(k, me).start()

        return carry

    lax.fori_loop(0, n_tm, send_d, 0)
    drecv[me] = dsend[...]

    @pl.when(me > 0)
    def _():
        for s in range(series_here):
            rim_copy(s).wait_recv()

    loads[2].wait()

    def produce(col0, width, s):
        cols = pl.ds(col0, width)
        raw[:, 0:width] = dot(tok[s], win[:, cols]).astype(BF16).astype(F32)
        for j in range(width // 128):
            lo = col0 + j * 128
            taps = convk_ref[:, lo : lo + 128] * 0.5
            bias = convb_ref[lo : lo + 128].reshape(1, 128) * 0.5

            def conv_body(c, carry):
                t0 = pl.multiple_of(c * Q + RIM - 8, 8)
                v = raw[pl.ds(t0, Q + 8), j * 128 : (j + 1) * 128]
                acc = v * taps[3:4]
                for back in range(1, KT):
                    acc = acc + pltpu.roll(v, back, 0) * taps[3 - back : 4 - back]
                h = acc[8:] + bias
                out = h + h * jnp.tanh(h)
                xs[s, pl.ds(pl.multiple_of(c * Q, 16), Q), lo : lo + 128] = out.astype(BF16)
                return carry

            lax.fori_loop(0, chunks, conv_body, 0)

    for s in range(series_here):
        produce(DI, 2 * N, s)

    def bt_body(ci, carry):
        s = ci // chunks
        t0 = pl.multiple_of((ci % chunks) * Q, 16)
        bt[ci] = xs[s, pl.ds(t0, Q), DI : DI + N].astype(F32).T.astype(BF16)
        return carry

    lax.fori_loop(0, nc, bt_body, 0)

    def i_copy(g, k, slot):
        return pltpu.make_async_remote_copy(
            src_ref=isend.at[g, k],
            dst_ref=irecv.at[g, slot],
            send_sem=i_ssem.at[g, k],
            recv_sem=i_rsem.at[g, slot],
            device_id=(k, ser),
            device_id_type=MESH,
        )

    def s_copy(g, k, slot):
        return pltpu.make_async_remote_copy(
            src_ref=ssend.at[g, k],
            dst_ref=srecv.at[g, slot],
            send_sem=s_ssem.at[g, k],
            recv_sem=s_rsem.at[g, slot],
            device_id=(k, ser),
            device_id_type=MESH,
        )

    def group(g):
        col0 = g * GC
        for s in range(series_here):
            produce(col0, GC, s)
            scur[s] = jnp.zeros((N, GC), F32)

            def inc_body(c, carry):
                ci = s * chunks + c
                t0 = pl.multiple_of(c * Q, 16)
                fx = dot(fhl[ci], eh[:, col0 : col0 + GC])
                wx = (xs[s, pl.ds(t0, Q), col0 : col0 + GC].astype(F32) * fx).astype(BF16)
                inc = dot(bt[ci], wx)
                cur = scur[s]
                sl[s, c, :, col0 : col0 + GC] = cur
                scur[s] = cur * rowx[pl.ds(ci, 1), col0 : col0 + GC] + inc
                return carry

            lax.fori_loop(0, chunks, inc_body, 0)
        parts = [scur[s].reshape(N // 8, 8, GC) for s in range(series_here)]
        isend[g] = jnp.concatenate(parts, axis=1).astype(BF16)

        @pl.when(me < n_tm - 1)
        def _():
            def send_i(k, carry):
                @pl.when(k != me)
                def _():
                    i_copy(g, k, me).start()

                return carry

            lax.fori_loop(0, n_tm, send_i, 0)

        irecv[g, me] = isend[g, me]

    def server(g):
        col0 = g * GC
        if g == 0:

            def wait_d(k, carry):
                @pl.when(k != me)
                def _():
                    d_copy(k, k).wait_recv()

                return carry

            lax.fori_loop(0, n_tm, wait_d, 0)
        dall = jnp.exp2(drecv[...].reshape(n_tm * 8, 128)[:, 0:H])
        dxs[...] = dot(hilo(dall), eh[:, col0 : col0 + GC]).reshape(n_tm, 8, GC)

        def emit(k, s0, s1):
            ssend[g, k] = jnp.concatenate([s0, s1], axis=0).astype(BF16)

            @pl.when((k != me) & (k > 0))
            def _():
                s_copy(g, k, me).start()

            @pl.when(k == me)
            def _():
                srecv[g, me] = jnp.concatenate([s0, s1], axis=0).astype(BF16)

        def scan_body(k, carry):
            s0, s1 = carry
            emit(k, s0, s1)

            @pl.when(k != me)
            def _():
                i_copy(g, k, k).wait_recv()

            part = irecv[g, k].astype(F32)
            s0 = s0 * dxs[k, 0:1, :] + part[0:8]
            s1 = s1 * dxs[k, 1:2, :] + part[8:16]
            return s0, s1

        zero = jnp.zeros((8, GC), F32)
        s0, s1 = lax.fori_loop(0, n_tm - 1, scan_body, (zero, zero))
        emit(n_tm - 1, s0, s1)

    def gates(s):
        def gate_body(i, carry):
            c0 = pl.multiple_of(i * 256, 256)
            h = dot(tok[s, RIM:, :], wgate[:, pl.ds(c0, 256)]) * 0.5
            sg[pl.ds(s * steps, steps), pl.ds(c0, 256)] = h + h * jnp.tanh(h)
            return carry

        lax.fori_loop(0, DI // 256, gate_body, 0)

    lanes1 = lax.broadcasted_iota(jnp.int32, (1, 128), 1)
    left = jnp.where(lanes1 < 64, 1.0, 0.0).astype(BF16)
    right = jnp.where(lanes1 < 64, 0.0, 1.0).astype(BF16)

    def intra(lo, hi):
        def intra_body(ci, carry):
            s = ci // chunks
            c = ci % chunks
            t0 = pl.multiple_of(c * Q, 16)
            r0 = pl.multiple_of(ci * Q, 16)
            cc = xs[s, pl.ds(t0, Q), DI + N : DI + 2 * N]
            sc = jnp.where(tri_r >= tri_c, dot(cc, bt[ci]), 0.0)
            for p in range(lo, hi):
                ws = []
                for h in (2 * p, 2 * p + 1):
                    d = cumc[ci, :, h : h + 1] - crt[ci, h : h + 1, :]
                    ws.append((jnp.exp2(jnp.minimum(d, 100.0)) * sc).astype(BF16))
                xp = xs[s, pl.ds(t0, Q), p * 128 : (p + 1) * 128]
                rhs = jnp.concatenate([xp * left, xp * right], axis=0)
                y = dot(jnp.concatenate(ws, axis=1), rhs)
                y = y + xp.astype(F32) * rowx[16:17, p * 128 : (p + 1) * 128]
                yb[pl.ds(r0, Q), p * 128 : (p + 1) * 128] = y
            return carry

        lax.fori_loop(0, nc, intra_body, 0)

    group(0)
    group(1)
    server(0)
    group(2)
    server(1)
    group(3)
    server(2)
    loads[3].wait()
    gates(0)
    server(3)
    gates(1)
    intra(0, H // 2)
    loads[4].wait()

    @pl.when(me == 0)
    def _():
        srecv[...] = jnp.zeros_like(srecv)

    for g in range(GROUPS):

        @pl.when(me > 0)
        def _():
            def wait_s(k, carry):
                @pl.when(k != me)
                def _():
                    s_copy(g, k, k).wait_recv()

                return carry

            lax.fori_loop(0, n_tm, wait_s, 0)

        got = srecv[g].astype(F32)
        for s in range(series_here):
            sin[s, :, g * GC : (g + 1) * GC] = got[:, 8 * s : 8 * s + 8, :].reshape(N, GC)

    def final_body(ci, carry):
        s = ci // chunks
        c = ci % chunks
        t0 = pl.multiple_of(c * Q, 16)
        r0 = pl.multiple_of(ci * Q, 16)
        cc = xs[s, pl.ds(t0, Q), DI + N : DI + 2 * N]
        ssq = jnp.zeros((Q, 128), F32)
        for g in range(2 * GROUPS):
            w = GC // 2
            cols = slice(g * w, (g + 1) * w)
            st = sin[s, :, cols] * rowx[pl.ds(8 + ci, 1), cols] + sl[s, c, :, cols]
            inter = dot(cc, st.astype(BF16))
            gx = dot(ghl[ci], eh[:, cols])
            y = yb[pl.ds(r0, Q), cols] + gx * inter
            gated = y * sg[pl.ds(r0, Q), cols]
            yb[pl.ds(r0, Q), cols] = gated
            sq = gated * gated
            for j in range(w // 128):
                ssq = ssq + sq[:, j * 128 : (j + 1) * 128]
        scale = lax.rsqrt(jnp.sum(ssq, axis=1, keepdims=True) * (1.0 / DI) + EPS)
        for j in range(DI // 256):
            cols = slice(j * 256, (j + 1) * 256)
            gain = gain_ref[cols].reshape(1, 256)
            nb[:, cols] = (yb[pl.ds(r0, Q), cols] * scale * gain).astype(BF16)
        live = jnp.where(lenv[s] > (me * steps + c * Q).astype(F32), 1.0, 0.0)[0:1, 0:1]
        res = dot(nb[...], wout[...]) * live
        o0 = pl.multiple_of(RIM + c * Q, 16)
        tok[s, pl.ds(o0, Q), :] = res.astype(BF16)
        pltpu.make_async_copy(
            tok.at[s, pl.ds(o0, Q), :], out_hbm.at[s, pl.ds(t0, Q), :], out_sem.at[ci]
        ).start()
        return carry

    lax.fori_loop(0, nc, final_body, 0)

    def drain_out(ci, carry):
        s = ci // chunks
        c = ci % chunks
        pltpu.make_async_copy(
            tok.at[s, pl.ds(pl.multiple_of(RIM + c * Q, 16), Q), :],
            out_hbm.at[s, pl.ds(pl.multiple_of(c * Q, 16), Q), :],
            out_sem.at[ci],
        ).wait()
        return carry

    lax.fori_loop(0, nc, drain_out, 0)

    def drain_len(k, carry):
        @pl.when(k != ser)
        def _():
            len_copy(k, ser).wait_send()

        return carry

    lax.fori_loop(0, n_ser, drain_len, 0)

    @pl.when(me < n_tm - 1)
    def _():
        for s in range(series_here):
            rim_copy(s).wait_send()

    def drain_tm(k, carry):
        @pl.when(k != me)
        def _():
            d_copy(k, me).wait_send()

        @pl.when((k != me) & (me < n_tm - 1))
        def _():
            for g in range(GROUPS):
                i_copy(g, k, me).wait_send()

        @pl.when((k != me) & (k > 0))
        def _():
            for g in range(GROUPS):
                s_copy(g, k, me).wait_send()

        return carry

    lax.fori_loop(0, n_tm, drain_tm, 0)


def body(
    n_tm,
    n_ser,
    tokens,
    gate_proj,
    input_proj,
    step_proj,
    conv_kernel,
    conv_bias,
    step_bias,
    decay_rate,
    skip_gain,
    norm_gain,
    out_proj,
    lengths,
    slot_series,
):
    series_here, steps, _ = tokens.shape
    chunks = steps // Q
    nc = series_here * chunks
    any_spec = pl.BlockSpec(memory_space=pl.ANY)
    vmem = pl.BlockSpec(memory_space=pltpu.VMEM)
    smem = pl.BlockSpec(memory_space=pltpu.SMEM)
    dma = pltpu.SemaphoreType.DMA
    scratch = [
        pltpu.VMEM((series_here, RIM + steps, D), BF16),
        pltpu.VMEM((D, W_IN), BF16),
        pltpu.VMEM((D, DI), BF16),
        pltpu.VMEM((DI, D), BF16),
        pltpu.VMEM((series_here, steps, W_IN), BF16),
        pltpu.VMEM((nc, N, Q), BF16),
        pltpu.VMEM((RIM + steps, GC), F32),
        pltpu.VMEM((nc, Q, H), F32),
        pltpu.VMEM((nc, H, Q), F32),
        pltpu.VMEM((nc, Q, 2 * H), BF16),
        pltpu.VMEM((nc, Q, 2 * H), BF16),
        pltpu.VMEM((2 * H, DI), BF16),
        pltpu.VMEM((32, H), F32),
        pltpu.VMEM((32, DI), F32),
        pltpu.VMEM((series_here, chunks, N, DI), F32),
        pltpu.VMEM((series_here, N, GC), F32),
        pltpu.VMEM((series_here, N, DI), F32),
        pltpu.VMEM((series_here * steps, DI), F32),
        pltpu.VMEM((series_here * steps, DI), F32),
        pltpu.VMEM((Q, DI), BF16),
        pltpu.VMEM((GROUPS, n_tm, 16, GC), BF16),
        pltpu.VMEM((GROUPS, n_tm, 16, GC), BF16),
        pltpu.VMEM((GROUPS, n_tm, 16, GC), BF16),
        pltpu.VMEM((GROUPS, n_tm, 16, GC), BF16),
        pltpu.VMEM((8, 128), F32),
        pltpu.VMEM((n_tm, 8, 128), F32),
        pltpu.VMEM((n_tm, 8, GC), F32),
        pltpu.VMEM((8, 128), jnp.int32),
        pltpu.VMEM((n_ser, 8, 128), jnp.int32),
        pltpu.VMEM((series_here, 8, 128), F32),
        dma((5,)),
        dma((nc,)),
        dma((n_ser,)),
        dma((n_ser,)),
        dma((series_here,)),
        dma((series_here,)),
        dma((n_tm,)),
        dma((n_tm,)),
        dma((GROUPS, n_tm)),
        dma((GROUPS, n_tm)),
        dma((GROUPS, n_tm)),
        dma((GROUPS, n_tm)),
    ]
    return pl.pallas_call(
        functools.partial(kernel, n_tm, n_ser, series_here, steps),
        out_shape=jax.ShapeDtypeStruct(tokens.shape, BF16),
        in_specs=[any_spec] * 3 + [vmem] * 7 + [any_spec] + [smem] * 2,
        out_specs=any_spec,
        scratch_shapes=scratch,
        compiler_params=pltpu.CompilerParams(
            collective_id=0,
            has_side_effects=True,
            vmem_limit_bytes=67_000_000,
        ),
        name="mixer",
    )(
        tokens,
        gate_proj,
        input_proj,
        step_proj,
        conv_kernel,
        conv_bias,
        step_bias,
        decay_rate,
        skip_gain,
        norm_gain,
        out_proj,
        lengths,
        slot_series,
    )


def solution(mesh):
    n_tm, n_ser = mesh.shape["tm"], mesh.shape["series"]
    in_specs = (P("series", "tm", None),) + (P(),) * 10 + (P("series"), P("series"))
    return jax.shard_map(
        functools.partial(body, n_tm, n_ser),
        mesh=mesh,
        in_specs=in_specs,
        out_specs=P("series", "tm", None),
        check_vma=False,
    )
```

time: 389 us -> 82.6 us (0.21)
  the two profiles are of different devices: /device:TPU:1 before, /device:TPU:16 now
where the time goes in v1:
time: 82.6 us; the launch traced here: 82.4 us
  Pallas kernels  77.6 us (94%)
  local copies, waits for them, and re-layouts  4.76 us (6%)
    pallas_call x1, Pallas kernels, body(): pl.pallas_call(functools.partial(kernel, n_tm, n_ser, series_here, steps)...  77.6 us
    unnamed x2, local copies, waits for them, and re-layouts  4.76 us

profile of v1, /device:TPU:16, one launch (start us, length us, event | category | flops | bytes accessed | tf_op | source)
XLA Modules:
  0.0 82.4 jit_solution(14141768331771027966)
XLA Ops:
  0.0 1.7 %copy.14.stepw_ref = bf16[1024,32]{1,0:T(8,128)(2,1)} copy(bf16[1024,32]{0,1:T(8,128)(2,1)} %param.16) | data formatting | bytes 131072 | tf_op args[3]
  1.7 77.6 %mixer.1 = bf16[2,512,1024]{2,1,0:T(8,128)(2,1)} custom-call(bf16[2,512,1024]{2,1,0:T(8,128)(2,1)} %tokens_hbm.1, bf16[1024,2048]{1,0:T(8,128)(2,1)} %gate_hbm.1, bf16[1024,2304]{1,0:T(8,128)(2,1)} %in_hbm.1, bf16[1024,32]{1,0:T(8,128)(2,1)} %copy.14.stepw_ref, f32[4,2304]{1,0:T(4,128)} %convk_ref.1, f32[2304]{0:T(1024)} %convb_ref.1, f32[32]{0:T(128)} %stepb_ref.1, ...), custom_call_target="tpu_custom_call" | custom-call | tf_op jit(solution)/shard_map/mixer/pallas_call | solution.py:630
  79.3 3.1 %copy.16 = bf16[2,512,1024]{2,1,0:T(8,128)(2,1)} copy(bf16[2,512,1024]{2,1,0:T(8,128)(2,1)} %mixer.1) | data formatting | bytes 4194304

commit v2 on v1

v2 whole, which is shorter than its diff:
```python
import functools
import math

import jax
import jax.numpy as jnp
from jax import lax
from jax.experimental import pallas as pl
from jax.experimental.pallas import tpu as pltpu
from jax.sharding import PartitionSpec as P

MESH = pl.DeviceIdType.MESH
F32 = jnp.float32
BF16 = jnp.bfloat16

D = 1024
DI = 2048
H = 32
N = 128
KT = 4
W_IN = DI + 2 * N
Q = 128
EPS = 1e-05
LOG2E = 1.4426950408889634
RIM = 16
GROUPS = 4
GC = DI // GROUPS
GATE_PIECES = 4
VMEM = 64_000_000


def dot(a, b, **kw):
    return jnp.dot(a, b, preferred_element_type=F32, **kw)


def scoped(name, f, *a):
    with jax.named_scope(name):
        return f(*a)


def expand(cols, first):
    lanes = lax.broadcasted_iota(jnp.int32, cols.shape, 1)
    index = jnp.where(lanes < 64, first, first + 1)
    return jnp.take_along_axis(cols, index, axis=1, mode="promise_in_bounds")


def kernel(
    n_tm,
    n_ser,
    series_here,
    steps,
    tokens_hbm,
    gate_hbm,
    in_hbm,
    stepw_ref,
    convk_ref,
    convb_ref,
    stepb_ref,
    rate_ref,
    skip_ref,
    gain_ref,
    out_w_hbm,
    len_smem,
    slot_smem,
    out_hbm,
    tok,
    win,
    wgate,
    wout,
    xs,
    bt,
    raw_a,
    raw_b,
    cumc,
    crt,
    scs,
    dts,
    rows,
    rowx,
    sl,
    ends,
    sin,
    ssq,
    ghl,
    eh,
    yb,
    sg,
    nb0,
    nb1,
    isend,
    irecv,
    ssend,
    srecv,
    dsend,
    drecv,
    dxs,
    lsend,
    lrecv,
    lenv,
    load_sem,
    out_sem,
    len_ssem,
    len_rsem,
    rim_ssem,
    rim_rsem,
    d_ssem,
    d_rsem,
    i_ssem,
    i_rsem,
    s_ssem,
    s_rsem,
):
    me = lax.axis_index("tm")
    ser = lax.axis_index("series")
    chunks = steps // Q
    nc = series_here * chunks
    nbs = (nb0, nb1)

    side = math.isqrt(n_tm)

    def away(d):
        x = lax.rem(me // side + d // side, side)
        return x * side + lax.rem(me + d, side)

    loads = []
    for s in range(series_here):
        loads.append(
            pltpu.make_async_copy(
                tokens_hbm.at[s], tok.at[s, pl.ds(RIM, steps), :], load_sem.at[s]
            )
        )
    loads.append(pltpu.make_async_copy(in_hbm, win, load_sem.at[2]))
    loads.append(pltpu.make_async_copy(out_w_hbm, wout, load_sem.at[3]))
    gate_loads = []
    for j in range(GATE_PIECES):
        gcols = pl.ds(j * (DI // GATE_PIECES), DI // GATE_PIECES)
        gate_loads.append(
            pltpu.make_async_copy(gate_hbm.at[:, gcols], wgate.at[:, gcols], load_sem.at[4 + j])
        )
    for c in [loads[0]] + gate_loads + loads[1:]:
        c.start()

    barrier = pltpu.get_barrier_semaphore()

    def greet_tm(k, carry):
        @pl.when(k != me)
        def _():
            pl.semaphore_signal(barrier, inc=1, device_id=(k, ser), device_id_type=MESH)

        return carry

    def greet_ser(k, carry):
        @pl.when(k != ser)
        def _():
            pl.semaphore_signal(barrier, inc=1, device_id=(me, k), device_id_type=MESH)

        return carry

    lax.fori_loop(0, n_tm, greet_tm, 0)
    lax.fori_loop(0, n_ser, greet_ser, 0)

    lane = lax.broadcasted_iota(jnp.int32, (8, 128), 1)
    lsend[...] = jnp.where(lane == 0, len_smem[0], jnp.where(lane == 1, len_smem[1], 0))
    er = lax.broadcasted_iota(jnp.int32, (2 * H, DI), 0)
    ec = lax.broadcasted_iota(jnp.int32, (2 * H, DI), 1)
    eh[...] = jnp.where((er % H) == ec // (DI // H), 1.0, 0.0).astype(BF16)
    dsend[...] = jnp.zeros_like(dsend)
    rows[...] = jnp.zeros_like(rows)

    def gates(s, lo, hi):
        for i in range(lo, hi):
            cols = slice(i * 256, (i + 1) * 256)
            if s == 0 and i % (DI // 256 // GATE_PIECES) == 0:
                gate_loads[i // (DI // 256 // GATE_PIECES)].wait()
            h = dot(tok[s, RIM:, :], wgate[:, cols]) * 0.5
            sg[s * steps : (s + 1) * steps, cols] = h + h * jnp.tanh(h)

    with jax.named_scope("barrier"):
        pl.semaphore_wait(barrier, n_tm + n_ser - 2)

    def len_copy(k, slot):
        return pltpu.make_async_remote_copy(
            src_ref=lsend,
            dst_ref=lrecv.at[slot],
            send_sem=len_ssem.at[0],
            recv_sem=len_rsem.at[0],
            device_id=(me, k),
            device_id_type=MESH,
        )

    def len_all():
        return pltpu.make_async_remote_copy(
            src_ref=lrecv.at[pl.ds(0, n_ser - 1)],
            dst_ref=lrecv.at[pl.ds(0, n_ser - 1)],
            send_sem=len_ssem.at[0],
            recv_sem=len_rsem.at[0],
            device_id=(me, ser),
            device_id_type=MESH,
        )

    def send_len(k, carry):
        @pl.when(k != ser)
        def _():
            len_copy(k, ser).start()

        return carry

    lax.fori_loop(0, n_ser, send_len, 0)
    lrecv[ser] = lsend[...]

    def rim_copy(s):
        return pltpu.make_async_remote_copy(
            src_ref=tokens_hbm.at[s, pl.ds(steps - RIM, RIM), :],
            dst_ref=tok.at[s, pl.ds(0, RIM), :],
            send_sem=rim_ssem.at[s],
            recv_sem=rim_rsem.at[s],
            device_id=(lax.rem(me + 1, n_tm), ser),
            device_id_type=MESH,
        )

    @pl.when(me < n_tm - 1)
    def _():
        for s in range(series_here):
            rim_copy(s).start()

    @pl.when(me == 0)
    def _():
        for s in range(series_here):
            tok[s, 0:RIM, :] = jnp.zeros((RIM, D), BF16)

    loads[0].wait()
    scoped("gates0", gates, 0, 0, 4)
    loads[1].wait()
    with jax.named_scope("lenwait"):
        len_all().wait_recv()
    for s in range(series_here):
        sid = slot_smem[s]
        found = jnp.zeros((8, 128), jnp.int32)
        for p in range(n_ser):
            hit = (lane < series_here) & (lane + series_here * p == sid)
            found = found + jnp.where(hit, lrecv[p], 0)
        lenv[s] = jnp.broadcast_to(
            jnp.sum(found.astype(F32), axis=1, keepdims=True), (8, 128)
        )

    tri_r = lax.broadcasted_iota(jnp.int32, (Q, Q), 0)
    tri_c = lax.broadcasted_iota(jnp.int32, (Q, Q), 1)

    def decays():
        eye = tri_r[0:H, 0:H] == tri_c[0:H, 0:H]

        def column(ref):
            wide = jnp.broadcast_to(ref[...].reshape(1, H), (H, H))
            return jnp.sum(jnp.where(eye, wide, 0.0), axis=1, keepdims=True)

        bias = column(stepb_ref)
        neg_rate = column(rate_ref) * (-LOG2E)
        for s in range(series_here):
            pre = lax.dot_general(
                stepw_ref[...],
                tok[s, RIM:, :],
                (((1,), (1,)), ((), ())),
                preferred_element_type=F32,
            )
            pre = pre + bias
            dt = jnp.maximum(pre, 0.0) + jnp.log1p(jnp.exp(-jnp.abs(pre)))
            for c in range(chunks):
                first = (me * steps + c * Q).astype(F32)
                live = jnp.where(lenv[s] > first, 1.0, 0.0)[0:1, :]
                ci = s * chunks + c
                dts[ci * H : (ci + 1) * H, :] = dt[:, c * Q : (c + 1) * Q] * live
        dt = dts[...]
        scaled = (dt.reshape(nc, H, Q) * neg_rate).reshape(nc * H, Q)
        upper = jnp.where(tri_r <= tri_c, 1.0, 0.0)
        cum = dot(scaled, upper, precision=lax.Precision.HIGHEST)
        lg = jnp.where(dt > 0.0, jnp.log(jnp.where(dt > 0.0, dt, 1.0)) * LOG2E, -1e30)
        crp = cum - lg
        crt[...] = crp.reshape(nc, H, Q)
        f = jnp.exp2(cum[:, Q - 1 : Q] - crp)
        g = jnp.exp2(cum)
        zero = jnp.zeros((128 - 3 * H, Q), F32)
        for ci in range(nc):
            r = slice(ci * H, (ci + 1) * H)
            col = jnp.concatenate([cum[r], f[r], g[r], zero], axis=0).T
            cumc[ci] = col
            high = col[:, 2 * H : 3 * H].astype(BF16)
            low = (col[:, 2 * H : 3 * H] - high.astype(F32)).astype(BF16)
            ghl[ci, :, 0:H] = high
            ghl[ci, :, H : 2 * H] = low

    scoped("decays", decays)

    r8 = lax.broadcasted_iota(jnp.int32, (8, H), 0)
    ecl = jnp.zeros((8, H), F32)
    ebef = jnp.zeros((8, H), F32)
    dtot = jnp.zeros((8, H), F32)
    for s in range(series_here):
        before = jnp.zeros((1, H), F32)
        for c in range(chunks):
            ci = s * chunks + c
            last = cumc[ci, Q - 1 : Q, 0:H]
            ecl = jnp.where(r8 == ci, jnp.exp2(last), ecl)
            ebef = jnp.where(r8 == ci, jnp.exp2(before), ebef)
            before = before + last
        dtot = jnp.where(r8 == s, before, dtot)
    dsend[:, 0:H] = dtot
    rows[0:8, 0:H] = ecl
    rows[8:16, 0:H] = ebef
    rows[16:24, 0:H] = jnp.broadcast_to(skip_ref[...].reshape(1, H), (8, H))
    for p in range(H // 2):
        rowx[:, p * 128 : (p + 1) * 128] = expand(rows[...], 2 * p)

    def to_peers(src, dst, ssem, rsem):
        def send(d, carry):
            k = away(d)
            pltpu.make_async_remote_copy(
                src_ref=src(k),
                dst_ref=dst.at[me],
                send_sem=ssem,
                recv_sem=rsem,
                device_id=(k, ser),
                device_id_type=MESH,
            ).start()
            return carry

        lax.fori_loop(1, n_tm, send, 0)

    def all_peers(dst, ssem, rsem):
        others = dst.at[pl.ds(0, n_tm - 1)]
        return pltpu.make_async_remote_copy(
            src_ref=others,
            dst_ref=others,
            send_sem=ssem,
            recv_sem=rsem,
            device_id=(me, ser),
            device_id_type=MESH,
        )

    d_all = all_peers(drecv, d_ssem.at[0], d_rsem.at[0])
    i_all = [all_peers(irecv.at[g], i_ssem.at[g], i_rsem.at[g]) for g in range(GROUPS)]
    s_all = [all_peers(srecv.at[g], s_ssem.at[g], s_rsem.at[g]) for g in range(GROUPS)]
    to_peers(lambda k: dsend, drecv, d_ssem.at[0], d_rsem.at[0])
    drecv[me] = dsend[...]

    @pl.when(me > 0)
    def _():
        for s in range(series_here):
            rim_copy(s).wait_recv()

    loads[2].wait()

    def project(raw, s, col0, at):
        raw[s, :, at : at + 256] = (
            dot(tok[s], win[:, col0 + at : col0 + at + 256]).astype(BF16).astype(F32)
        )

    def convolve(raw, s, col0, at):
        lo = col0 + at
        taps = convk_ref[:, lo : lo + 128] * 0.5
        bias = convb_ref[lo : lo + 128].reshape(1, 128) * 0.5
        for c in range(chunks):
            t0 = c * Q
            v = raw[s, t0 + RIM - 8 : t0 + RIM + Q, at : at + 128]
            acc = v * taps[3:4]
            for back in range(1, KT):
                acc = acc + pltpu.roll(v, back, 0) * taps[3 - back : 4 - back]
            h = acc[8:] + bias
            xs[s, t0 : t0 + Q, lo : lo + 128] = (h + h * jnp.tanh(h)).astype(BF16)

    def lead():
        for s in range(series_here):
            project(raw_b, s, DI, 0)
        for s in range(series_here):
            for half in range(2):
                project(raw_a, s, 0, half * 256)
                convolve(raw_b, s, DI, half * 128)
            for c in range(chunks):
                ci = s * chunks + c
                b = xs[s, c * Q : (c + 1) * Q, DI : DI + N]
                bt[ci] = b.astype(F32).T.astype(BF16)
                cc = xs[s, c * Q : (c + 1) * Q, DI + N : DI + 2 * N]
                scs[ci] = jnp.where(tri_r >= tri_c, dot(cc, bt[ci]), 0.0)

    scoped("lead", lead)

    def group(g):
        col0 = g * GC
        here, ahead = (raw_a, raw_b) if g % 2 == 0 else (raw_b, raw_a)
        for s in range(series_here):
            for half in range(2):
                at = half * 256
                if g + 1 < GROUPS:
                    project(ahead, s, col0 + GC, at)
                else:
                    gates(0, 4 + 2 * s + half, 5 + 2 * s + half)
                for j in range(2):
                    convolve(here, s, col0, at + j * 128)
                hcols = slice(col0 + at, col0 + at + 256)
                for c in range(chunks):
                    ci = s * chunks + c
                    head = (col0 + at) // 64
                    fx = jnp.concatenate(
                        [expand(cumc[ci], H + head + 2 * j) for j in range(2)], axis=1
                    )
                    x = xs[s, c * Q : (c + 1) * Q, hcols].astype(F32)
                    inc = dot(bt[ci], (x * fx).astype(BF16))
                    if c > 0:
                        inc = inc + sl[s, c - 1, :, hcols] * rowx[ci : ci + 1, hcols]
                    if c + 1 < chunks:
                        sl[s, c, :, hcols] = inc
                    else:
                        ends[s, :, at : at + 256] = inc
        parts = [ends[s].reshape(N // 8, 8, GC) for s in range(series_here)]
        isend[g] = jnp.concatenate(parts, axis=1).astype(BF16)

        to_peers(lambda k: isend.at[g, k], irecv.at[g], i_ssem.at[g], i_rsem.at[g])
        irecv[g, me] = isend[g, me]

    def server(g):
        col0 = g * GC
        if g == 0:
            d_all.wait_recv()
        dall = jnp.exp2(drecv[...].reshape(n_tm * 8, 128))
        for j in range(GC // 128):
            wide = expand(dall, (col0 + j * 128) // 64)
            dxs[:, :, j * 128 : (j + 1) * 128] = wide.reshape(n_tm, 8, 128)

        i_all[g].wait_recv()
        s0 = s1 = jnp.zeros((8, GC), F32)
        for k in range(n_tm):
            ssend[g, k] = jnp.concatenate([s0, s1], axis=0).astype(BF16)
            if k + 1 < n_tm:
                part = irecv[g, k].astype(F32)
                s0 = s0 * dxs[k, 0:1, :] + part[0:8]
                s1 = s1 * dxs[k, 1:2, :] + part[8:16]
        srecv[g, me] = ssend[g, me]
        to_peers(lambda k: ssend.at[g, k], srecv.at[g], s_ssem.at[g], s_rsem.at[g])

    lanes1 = lax.broadcasted_iota(jnp.int32, (1, 128), 1)
    left = jnp.where(lanes1 < 64, 1.0, 0.0).astype(BF16)
    right = jnp.where(lanes1 < 64, 0.0, 1.0).astype(BF16)

    def intra(lo, hi):
        def intra_chunk(ci):
            s = ci // chunks
            t0 = pl.multiple_of((ci % chunks) * Q, 16)
            r0 = pl.multiple_of(ci * Q, 16)
            for p in range(H // 2):
                ws = []
                for h in (2 * p, 2 * p + 1):
                    d = cumc[ci, :, h : h + 1] - crt[ci, h : h + 1, :]
                    ws.append((jnp.exp2(jnp.minimum(d, 100.0)) * scs[ci]).astype(BF16))
                xp = xs[s, pl.ds(t0, Q), p * 128 : (p + 1) * 128]
                rhs = jnp.concatenate([xp * left, xp * right], axis=0)
                y = dot(jnp.concatenate(ws, axis=1), rhs)
                y = y + xp.astype(F32) * rowx[16:17, p * 128 : (p + 1) * 128]
                yb[pl.ds(r0, Q), p * 128 : (p + 1) * 128] = y

        def intra_body(i, carry):
            for half in range(2):
                g0 = pl.multiple_of((2 * i + half) * 256, 256)
                h = dot(tok[1, RIM:, :], wgate[:, pl.ds(g0, 256)]) * 0.5
                sg[steps : 2 * steps, pl.ds(g0, 256)] = h + h * jnp.tanh(h)
                intra_chunk(2 * i + half)
            return carry

        lax.fori_loop(lo, hi, intra_body, 0)

    scoped("group0", group, 0)
    scoped("group1", group, 1)
    scoped("group2", group, 2)
    scoped("server0", server, 0)
    scoped("group3", group, 3)
    scoped("server1", server, 1)
    scoped("intra0", intra, 0, nc // 4)
    scoped("server2", server, 2)
    scoped("intra1", intra, nc // 4, nc // 2)
    scoped("server3", server, 3)
    loads[3].wait()

    def arrive(g):
        s_all[g].wait_recv()
        got = srecv[g].astype(F32)
        for s in range(series_here):
            sin[s] = got[:, 8 * s : 8 * s + 8, :].reshape(N, GC)

    def mix(g, s, c):
        ci = s * chunks + c
        r = slice(ci * Q, (ci + 1) * Q)
        cc = xs[s, c * Q : (c + 1) * Q, DI + N : DI + 2 * N]
        total = None if g == 0 else ssq[r, :]
        for half in range(2):
            at = half * 256
            cols = slice(g * GC + at, g * GC + at + 256)
            st = sin[s, :, at : at + 256]
            if c > 0:
                st = st * rowx[8 + ci : 9 + ci, cols] + sl[s, c - 1, :, cols]
            inter = dot(cc, st.astype(BF16))
            gx = dot(ghl[ci], eh[:, cols])
            gated = (yb[r, cols] + gx * inter) * sg[r, cols]
            gain = gain_ref[cols].reshape(1, 256)
            nbs[s][c * Q : (c + 1) * Q, at : at + 256] = (gated * gain).astype(BF16)
            sq = gated * gated
            for j in range(2):
                piece = sq[:, j * 128 : (j + 1) * 128]
                total = piece if total is None else total + piece
        ssq[r, :] = total

    def row_scale(s):
        rs = slice(s * steps, (s + 1) * steps)
        mean = jnp.sum(ssq[rs, :], axis=1, keepdims=True) * (1.0 / DI)
        scale = lax.rsqrt(mean + EPS)
        for c in range(chunks):
            live = jnp.where(lenv[s] > (me * steps + c * Q).astype(F32), 1.0, 0.0)[0:1, 0:1]
            piece = scale[c * Q : (c + 1) * Q] * live
            ssq[s * steps + c * Q : s * steps + (c + 1) * Q, :] = jnp.broadcast_to(piece, (Q, 128))

    def leave(g, s, n):
        acc = raw_a if n < 2 else raw_b
        at = (n % 2) * 256
        part = dot(nbs[s][...], wout[g * GC : (g + 1) * GC, n * 256 : (n + 1) * 256])
        if g > 0:
            part = part + acc[s, 0:steps, at : at + 256]
        if g < GROUPS - 1:
            acc[s, 0:steps, at : at + 256] = part
            return
        for j in range(2):
            res = part[:, j * 128 : (j + 1) * 128] * ssq[s * steps : (s + 1) * steps, :]
            lo = n * 256 + j * 128
            tok[s, RIM : RIM + steps, lo : lo + 128] = res.astype(BF16)

    def out_copy(s):
        return pltpu.make_async_copy(
            tok.at[s, pl.ds(RIM, steps), :], out_hbm.at[s], out_sem.at[s]
        )

    for g in range(GROUPS):
        scoped("arrive", arrive, g)
        with jax.named_scope("final"):
            for c in range(chunks):
                mix(g, 0, c)
                if g > 0:
                    leave(g - 1, 1, c)
            if g == GROUPS - 1:
                row_scale(0)
            for c in range(chunks):
                mix(g, 1, c)
                leave(g, 0, c)
    out_copy(0).start()
    with jax.named_scope("last"):
        row_scale(1)
        for c in range(chunks):
            leave(GROUPS - 1, 1, c)
    out_copy(1).start()

    with jax.named_scope("drain"):
        for s in range(series_here):
            out_copy(s).wait()

    len_all().wait_send()

    @pl.when(me < n_tm - 1)
    def _():
        for s in range(series_here):
            rim_copy(s).wait_send()

    d_all.wait_send()
    for g in range(GROUPS):
        i_all[g].wait_send()
        s_all[g].wait_send()


def body(
    n_tm,
    n_ser,
    tokens,
    gate_proj,
    input_proj,
    step_proj,
    conv_kernel,
    conv_bias,
    step_bias,
    decay_rate,
    skip_gain,
    norm_gain,
    out_proj,
    lengths,
    slot_series,
):
    series_here, steps, _ = tokens.shape
    chunks = steps // Q
    nc = series_here * chunks
    any_spec = pl.BlockSpec(memory_space=pl.ANY)
    vmem = pl.BlockSpec(memory_space=pltpu.VMEM)
    smem = pl.BlockSpec(memory_space=pltpu.SMEM)
    dma = pltpu.SemaphoreType.DMA
    scratch = [
        pltpu.VMEM((series_here, RIM + steps, D), BF16),
        pltpu.VMEM((D, W_IN), BF16),
        pltpu.VMEM((D, DI), BF16),
        pltpu.VMEM((DI, D), BF16),
        pltpu.VMEM((series_here, steps, W_IN), BF16),
        pltpu.VMEM((nc, N, Q), BF16),
        pltpu.VMEM((series_here, RIM + steps, GC), F32),
        pltpu.VMEM((series_here, RIM + steps, GC), F32),
        pltpu.VMEM((nc, Q, 128), F32),
        pltpu.VMEM((nc, H, Q), F32),
        pltpu.VMEM((nc, Q, Q), F32),
        pltpu.VMEM((nc * H, Q), F32),
        pltpu.VMEM((24, 128), F32),
        pltpu.VMEM((24, DI), F32),
        pltpu.VMEM((series_here, chunks - 1, N, DI), F32),
        pltpu.VMEM((series_here, N, GC), F32),
        pltpu.VMEM((series_here, N, GC), F32),
        pltpu.VMEM((series_here * steps, 128), F32),
        pltpu.VMEM((nc, Q, 2 * H), BF16),
        pltpu.VMEM((2 * H, DI), BF16),
        pltpu.VMEM((series_here * steps, DI), F32),
        pltpu.VMEM((series_here * steps, DI), F32),
        pltpu.VMEM((steps, GC), BF16),
        pltpu.VMEM((steps, GC), BF16),
        pltpu.VMEM((GROUPS, n_tm, 16, GC), BF16),
        pltpu.VMEM((GROUPS, n_tm, 16, GC), BF16),
        pltpu.VMEM((GROUPS, n_tm, 16, GC), BF16),
        pltpu.VMEM((GROUPS, n_tm, 16, GC), BF16),
        pltpu.VMEM((8, 128), F32),
        pltpu.VMEM((n_tm, 8, 128), F32),
        pltpu.VMEM((n_tm, 8, GC), F32),
        pltpu.VMEM((8, 128), jnp.int32),
        pltpu.VMEM((n_ser, 8, 128), jnp.int32),
        pltpu.VMEM((series_here, 8, 128), F32),
        dma((4 + GATE_PIECES,)),
        dma((nc,)),
        dma((1,)),
        dma((1,)),
        dma((series_here,)),
        dma((series_here,)),
        dma((1,)),
        dma((1,)),
        dma((GROUPS,)),
        dma((GROUPS,)),
        dma((GROUPS,)),
        dma((GROUPS,)),
    ]
    return pl.pallas_call(
        functools.partial(kernel, n_tm, n_ser, series_here, steps),
        out_shape=jax.ShapeDtypeStruct(tokens.shape, BF16),
        in_specs=[any_spec] * 3 + [vmem] * 7 + [any_spec] + [smem] * 2,
        out_specs=any_spec,
        scratch_shapes=scratch,
        compiler_params=pltpu.CompilerParams(
            collective_id=0,
            has_side_effects=True,
            vmem_limit_bytes=VMEM,
        ),
        name="mixer",
    )(
        tokens,
        gate_proj,
        input_proj,
        step_proj.T,
        conv_kernel,
        conv_bias,
        step_bias,
        decay_rate,
        skip_gain,
        norm_gain,
        out_proj,
        lengths,
        slot_series,
    )


def solution(mesh):
    n_tm, n_ser = mesh.shape["tm"], mesh.shape["series"]
    in_specs = (P("series", "tm", None),) + (P(),) * 10 + (P("series"), P("series"))
    return jax.shard_map(
        functools.partial(body, n_tm, n_ser),
        mesh=mesh,
        in_specs=in_specs,
        out_specs=P("series", "tm", None),
        check_vma=False,
    )
```

time: 82.6 us -> 52.2 us (0.63)
  the two profiles are of different devices: /device:TPU:16 before, /device:TPU:1 now
where the time goes in v2:
time: 52.2 us; the launch traced here: 52 us
  Pallas kernels  48.9 us (94%)
  local copies, waits for them, and re-layouts  3.08 us (6%)
    pallas_call x1, Pallas kernels, body(): pl.pallas_call(functools.partial(kernel, n_tm, n_ser, series_here, steps)...  48.9 us
    unnamed x1, local copies, waits for them, and re-layouts  3.08 us

profile of v2, /device:TPU:1, one launch (start us, length us, event | category | flops | bytes accessed | tf_op | source)
XLA Modules:
  0.0 52.0 jit_solution(1239905080930167120)
XLA Ops:
  0.0 48.9 %mixer.1 = bf16[2,512,1024]{2,1,0:T(8,128)(2,1)} custom-call(bf16[2,512,1024]{2,1,0:T(8,128)(2,1)} %tokens_hbm.1, bf16[1024,2048]{1,0:T(8,128)(2,1)} %gate_hbm.1, bf16[1024,2304]{1,0:T(8,128)(2,1)} %in_hbm.1, bf16[32,1024]{1,0:T(8,128)(2,1)} %bitcast.1, f32[4,2304]{1,0:T(4,128)} %convk_ref.1, f32[2304]{0:T(1024)} %convb_ref.1, f32[32]{0:T(128)} %stepb_ref.1, ...), custom_call_target="tpu_custom_call" | custom-call | tf_op jit(solution)/shard_map/mixer/pallas_call | solution.py:644
  48.9 3.1 %copy.15 = bf16[2,512,1024]{2,1,0:T(8,128)(2,1)} copy(bf16[2,512,1024]{2,1,0:T(8,128)(2,1)} %mixer.1) | data formatting | bytes 4194304

commit v3 on v2

--- a/solution.py
+++ b/solution.py
@@ -61,7 +61,7 @@
     out_w_hbm,
     len_smem,
     slot_smem,
-    out_hbm,
+    out_ref,
     tok,
     win,
     wgate,
@@ -97,7 +97,6 @@
     lrecv,
     lenv,
     load_sem,
-    out_sem,
     len_ssem,
     len_rsem,
     rim_ssem,
@@ -227,9 +226,33 @@
         for s in range(series_here):
             tok[s, 0:RIM, :] = jnp.zeros((RIM, D), BF16)
 
+    tri_r = lax.broadcasted_iota(jnp.int32, (Q, Q), 0)
+    tri_c = lax.broadcasted_iota(jnp.int32, (Q, Q), 1)
+
+    def column(ref):
+        wide = jnp.broadcast_to(ref[...].reshape(1, H), (H, H))
+        eye = tri_r[0:H, 0:H] == tri_c[0:H, 0:H]
+        return jnp.sum(jnp.where(eye, wide, 0.0), axis=1, keepdims=True)
+
+    def softplus():
+        bias = column(stepb_ref)
+        for s in range(series_here):
+            pre = lax.dot_general(
+                stepw_ref[...],
+                tok[s, RIM:, :],
+                (((1,), (1,)), ((), ())),
+                preferred_element_type=F32,
+            )
+            pre = pre + bias
+            dt = jnp.maximum(pre, 0.0) + jnp.log1p(jnp.exp(-jnp.abs(pre)))
+            for c in range(chunks):
+                ci = s * chunks + c
+                dts[ci * H : (ci + 1) * H, :] = dt[:, c * Q : (c + 1) * Q]
+
     loads[0].wait()
     scoped("gates0", gates, 0, 0, 4)
     loads[1].wait()
+    scoped("softplus", softplus)
     with jax.named_scope("lenwait"):
         len_all().wait_recv()
     for s in range(series_here):
@@ -242,32 +265,14 @@
             jnp.sum(found.astype(F32), axis=1, keepdims=True), (8, 128)
         )
 
-    tri_r = lax.broadcasted_iota(jnp.int32, (Q, Q), 0)
-    tri_c = lax.broadcasted_iota(jnp.int32, (Q, Q), 1)
-
     def decays():
-        eye = tri_r[0:H, 0:H] == tri_c[0:H, 0:H]
-
-        def column(ref):
-            wide = jnp.broadcast_to(ref[...].reshape(1, H), (H, H))
-            return jnp.sum(jnp.where(eye, wide, 0.0), axis=1, keepdims=True)
-
-        bias = column(stepb_ref)
-        neg_rate = column(rate_ref) * (-LOG2E)
-        for s in range(series_here):
-            pre = lax.dot_general(
-                stepw_ref[...],
-                tok[s, RIM:, :],
-                (((1,), (1,)), ((), ())),
-                preferred_element_type=F32,
-            )
-            pre = pre + bias
-            dt = jnp.maximum(pre, 0.0) + jnp.log1p(jnp.exp(-jnp.abs(pre)))
+        for s in range(series_here):
             for c in range(chunks):
                 first = (me * steps + c * Q).astype(F32)
                 live = jnp.where(lenv[s] > first, 1.0, 0.0)[0:1, :]
-                ci = s * chunks + c
-                dts[ci * H : (ci + 1) * H, :] = dt[:, c * Q : (c + 1) * Q] * live
+                r = slice((s * chunks + c) * H, (s * chunks + c + 1) * H)
+                dts[r, :] = dts[r, :] * live
+        neg_rate = column(rate_ref) * (-LOG2E)
         dt = dts[...]
         scaled = (dt.reshape(nc, H, Q) * neg_rate).reshape(nc * H, Q)
         upper = jnp.where(tri_r <= tri_c, 1.0, 0.0)
@@ -526,12 +531,7 @@
         for j in range(2):
             res = part[:, j * 128 : (j + 1) * 128] * ssq[s * steps : (s + 1) * steps, :]
             lo = n * 256 + j * 128
-            tok[s, RIM : RIM + steps, lo : lo + 128] = res.astype(BF16)
-
-    def out_copy(s):
-        return pltpu.make_async_copy(
-            tok.at[s, pl.ds(RIM, steps), :], out_hbm.at[s], out_sem.at[s]
-        )
+            out_ref[s, :, lo : lo + 128] = res.astype(BF16)
 
     for g in range(GROUPS):
         scoped("arrive", arrive, g)
@@ -545,16 +545,10 @@
             for c in range(chunks):
                 mix(g, 1, c)
                 leave(g, 0, c)
-    out_copy(0).start()
     with jax.named_scope("last"):
         row_scale(1)
         for c in range(chunks):
             leave(GROUPS - 1, 1, c)
-    out_copy(1).start()
-
-    with jax.named_scope("drain"):
-        for s in range(series_here):
-            out_copy(s).wait()
 
     len_all().wait_send()
 
@@ -629,7 +623,6 @@
         pltpu.VMEM((n_ser, 8, 128), jnp.int32),
         pltpu.VMEM((series_here, 8, 128), F32),
         dma((4 + GATE_PIECES,)),
-        dma((nc,)),
         dma((1,)),
         dma((1,)),
         dma((series_here,)),
@@ -643,9 +636,9 @@
     ]
     return pl.pallas_call(
         functools.partial(kernel, n_tm, n_ser, series_here, steps),
-        out_shape=jax.ShapeDtypeStruct(tokens.shape, BF16),
+        out_shape=pltpu.VMEM(tokens.shape, BF16),
         in_specs=[any_spec] * 3 + [vmem] * 7 + [any_spec] + [smem] * 2,
-        out_specs=any_spec,
+        out_specs=vmem,
         scratch_shapes=scratch,
         compiler_params=pltpu.CompilerParams(
             collective_id=0,

time: 52.2 us -> 48.6 us (0.931)
  Pallas kernels: 48.9 us -> 47.1 us
  local copies, waits for them, and re-layouts: 3.08 us -> 1.32 us
    pallas_call x1, Pallas kernels: 48.9 us -> 47.1 us  [body(): pl.pallas_call(functools.partial(kernel, n_tm, n_ser, series_here, steps)...]
    unnamed x1, local copies, waits for them, and re-layouts: 3.08 us -> 1.32 us
where the time goes in v3:
time: 48.6 us; the launch traced here: 48.5 us
  Pallas kernels  47.1 us (97%)
  local copies, waits for them, and re-layouts  1.32 us (3%)
    pallas_call x1, Pallas kernels, body(): pl.pallas_call(functools.partial(kernel, n_tm, n_ser, series_here, steps)...  47.1 us
    unnamed x1, local copies, waits for them, and re-layouts  1.32 us

profile of v3, /device:TPU:1, one launch (start us, length us, event | category | flops | bytes accessed | tf_op | source)
XLA Modules:
  0.0 48.5 jit_solution(14521274660412745984)
XLA Ops:
  0.0 47.1 %mixer.1 = bf16[2,512,1024]{2,1,0:T(8,128)(2,1)S(1)} custom-call(bf16[2,512,1024]{2,1,0:T(8,128)(2,1)} %tokens_hbm.1, bf16[1024,2048]{1,0:T(8,128)(2,1)} %gate_hbm.1, bf16[1024,2304]{1,0:T(8,128)(2,1)} %in_hbm.1, bf16[32,1024]{1,0:T(8,128)(2,1)} %bitcast.1, f32[4,2304]{1,0:T(4,128)} %convk_ref.1, f32[2304]{0:T(1024)} %convb_ref.1, f32[32]{0:T(128)} %stepb_ref.1, ...), custom_call_target="tpu_custom_call" | custom-call | tf_op jit(solution)/shard_map/mixer/pallas_call | solution.py:637
  47.2 1.3 %copy.15 = bf16[2,512,1024]{2,1,0:T(8,128)(2,1)} copy(bf16[2,512,1024]{2,1,0:T(8,128)(2,1)S(1)} %mixer.1) | data formatting | bytes 4194304

commit v4 on v3

--- a/solution.py
+++ b/solution.py
@@ -22,6 +22,7 @@
 EPS = 1e-05
 LOG2E = 1.4426950408889634
 RIM = 16
+SENT = 8
 GROUPS = 4
 GC = DI // GROUPS
 GATE_PIECES = 4
@@ -116,6 +117,8 @@
 
     side = math.isqrt(n_tm)
 
+    origin = me // n_tm
+
     def away(d):
         x = lax.rem(me // side + d // side, side)
         return x * side + lax.rem(me + d, side)
@@ -135,7 +138,7 @@
         gate_loads.append(
             pltpu.make_async_copy(gate_hbm.at[:, gcols], wgate.at[:, gcols], load_sem.at[4 + j])
         )
-    for c in [loads[0]] + gate_loads + loads[1:]:
+    for c in loads[:2] + gate_loads + loads[2:]:
         c.start()
 
     barrier = pltpu.get_barrier_semaphore()
@@ -208,14 +211,18 @@
 
     def rim_copy(s):
         return pltpu.make_async_remote_copy(
-            src_ref=tokens_hbm.at[s, pl.ds(steps - RIM, RIM), :],
-            dst_ref=tok.at[s, pl.ds(0, RIM), :],
+            src_ref=tok.at[s, pl.ds(RIM + steps - SENT, SENT), :],
+            dst_ref=tok.at[s, pl.ds(RIM - SENT, SENT), :],
             send_sem=rim_ssem.at[s],
             recv_sem=rim_rsem.at[s],
             device_id=(lax.rem(me + 1, n_tm), ser),
             device_id_type=MESH,
         )
 
+    for s in range(series_here):
+        loads[s].wait()
+        tok[s, 0 : RIM - SENT, :] = jnp.zeros((RIM - SENT, D), BF16)
+
     @pl.when(me < n_tm - 1)
     def _():
         for s in range(series_here):
@@ -224,7 +231,7 @@
     @pl.when(me == 0)
     def _():
         for s in range(series_here):
-            tok[s, 0:RIM, :] = jnp.zeros((RIM, D), BF16)
+            tok[s, RIM - SENT : RIM, :] = jnp.zeros((SENT, D), BF16)
 
     tri_r = lax.broadcasted_iota(jnp.int32, (Q, Q), 0)
     tri_c = lax.broadcasted_iota(jnp.int32, (Q, Q), 1)
@@ -249,22 +256,8 @@
                 ci = s * chunks + c
                 dts[ci * H : (ci + 1) * H, :] = dt[:, c * Q : (c + 1) * Q]
 
-    loads[0].wait()
     scoped("gates0", gates, 0, 0, 4)
-    loads[1].wait()
     scoped("softplus", softplus)
-    with jax.named_scope("lenwait"):
-        len_all().wait_recv()
-    for s in range(series_here):
-        sid = slot_smem[s]
-        found = jnp.zeros((8, 128), jnp.int32)
-        for p in range(n_ser):
-            hit = (lane < series_here) & (lane + series_here * p == sid)
-            found = found + jnp.where(hit, lrecv[p], 0)
-        lenv[s] = jnp.broadcast_to(
-            jnp.sum(found.astype(F32), axis=1, keepdims=True), (8, 128)
-        )
-
     def decays():
         for s in range(series_here):
             for c in range(chunks):
@@ -292,27 +285,26 @@
             ghl[ci, :, 0:H] = high
             ghl[ci, :, H : 2 * H] = low
 
-    scoped("decays", decays)
-
-    r8 = lax.broadcasted_iota(jnp.int32, (8, H), 0)
-    ecl = jnp.zeros((8, H), F32)
-    ebef = jnp.zeros((8, H), F32)
-    dtot = jnp.zeros((8, H), F32)
-    for s in range(series_here):
-        before = jnp.zeros((1, H), F32)
-        for c in range(chunks):
-            ci = s * chunks + c
-            last = cumc[ci, Q - 1 : Q, 0:H]
-            ecl = jnp.where(r8 == ci, jnp.exp2(last), ecl)
-            ebef = jnp.where(r8 == ci, jnp.exp2(before), ebef)
-            before = before + last
-        dtot = jnp.where(r8 == s, before, dtot)
-    dsend[:, 0:H] = dtot
-    rows[0:8, 0:H] = ecl
-    rows[8:16, 0:H] = ebef
-    rows[16:24, 0:H] = jnp.broadcast_to(skip_ref[...].reshape(1, H), (8, H))
-    for p in range(H // 2):
-        rowx[:, p * 128 : (p + 1) * 128] = expand(rows[...], 2 * p)
+    def row_values():
+        r8 = lax.broadcasted_iota(jnp.int32, (8, H), 0)
+        ecl = jnp.zeros((8, H), F32)
+        ebef = jnp.zeros((8, H), F32)
+        dtot = jnp.zeros((8, H), F32)
+        for s in range(series_here):
+            before = jnp.zeros((1, H), F32)
+            for c in range(chunks):
+                ci = s * chunks + c
+                last = cumc[ci, Q - 1 : Q, 0:H]
+                ecl = jnp.where(r8 == ci, jnp.exp2(last), ecl)
+                ebef = jnp.where(r8 == ci, jnp.exp2(before), ebef)
+                before = before + last
+            dtot = jnp.where(r8 == s, before, dtot)
+        dsend[:, 0:H] = dtot
+        rows[0:8, 0:H] = ecl
+        rows[8:16, 0:H] = ebef
+        rows[16:24, 0:H] = jnp.broadcast_to(skip_ref[...].reshape(1, H), (8, H))
+        for p in range(H // 2):
+            rowx[:, p * 128 : (p + 1) * 128] = expand(rows[...], 2 * p)
 
     def to_peers(src, dst, ssem, rsem):
         def send(d, carry):
@@ -343,20 +335,21 @@
     d_all = all_peers(drecv, d_ssem.at[0], d_rsem.at[0])
     i_all = [all_peers(irecv.at[g], i_ssem.at[g], i_rsem.at[g]) for g in range(GROUPS)]
     s_all = [all_peers(srecv.at[g], s_ssem.at[g], s_rsem.at[g]) for g in range(GROUPS)]
-    to_peers(lambda k: dsend, drecv, d_ssem.at[0], d_rsem.at[0])
-    drecv[me] = dsend[...]
-
-    @pl.when(me > 0)
-    def _():
-        for s in range(series_here):
-            rim_copy(s).wait_recv()
-
-    loads[2].wait()
+
+    with jax.named_scope("rimwait"):
+
+        @pl.when(me > 0)
+        def _():
+            for s in range(series_here):
+                rim_copy(s).wait_recv()
+
+    with jax.named_scope("winwait"):
+        loads[2].wait()
 
     def project(raw, s, col0, at):
-        raw[s, :, at : at + 256] = (
-            dot(tok[s], win[:, col0 + at : col0 + at + 256]).astype(BF16).astype(F32)
-        )
+        got = dot(tok[s], win[:, col0 + at : col0 + at + 256]).astype(BF16).astype(F32)
+        for j in range(2):
+            raw[s, at // 128 + j] = got[:, j * 128 : (j + 1) * 128]
 
     def convolve(raw, s, col0, at):
         lo = col0 + at
@@ -364,11 +357,10 @@
         bias = convb_ref[lo : lo + 128].reshape(1, 128) * 0.5
         for c in range(chunks):
             t0 = c * Q
-            v = raw[s, t0 + RIM - 8 : t0 + RIM + Q, at : at + 128]
-            acc = v * taps[3:4]
-            for back in range(1, KT):
-                acc = acc + pltpu.roll(v, back, 0) * taps[3 - back : 4 - back]
-            h = acc[8:] + bias
+            h = bias
+            for k in range(KT):
+                v = raw[s, at // 128, pl.ds(origin + (t0 + RIM - KT + 1 + k), Q), :]
+                h = h + v * taps[k : k + 1]
             xs[s, t0 : t0 + Q, lo : lo + 128] = (h + h * jnp.tanh(h)).astype(BF16)
 
     def lead():
@@ -386,10 +378,25 @@
                 scs[ci] = jnp.where(tri_r >= tri_c, dot(cc, bt[ci]), 0.0)
 
     scoped("lead", lead)
+    with jax.named_scope("lenwait"):
+        len_all().wait_recv()
+    for s in range(series_here):
+        sid = slot_smem[s]
+        found = jnp.zeros((8, 128), jnp.int32)
+        for p in range(n_ser):
+            hit = (lane < series_here) & (lane + series_here * p == sid)
+            found = found + jnp.where(hit, lrecv[p], 0)
+        lenv[s] = jnp.broadcast_to(
+            jnp.sum(found.astype(F32), axis=1, keepdims=True), (8, 128)
+        )
+
 
     def group(g):
         col0 = g * GC
         here, ahead = (raw_a, raw_b) if g % 2 == 0 else (raw_b, raw_a)
+        if g == 0:
+            decays()
+            row_values()
         for s in range(series_here):
             for half in range(2):
                 at = half * 256
@@ -417,6 +424,9 @@
         parts = [ends[s].reshape(N // 8, 8, GC) for s in range(series_here)]
         isend[g] = jnp.concatenate(parts, axis=1).astype(BF16)
 
+        if g == 0:
+            to_peers(lambda k: dsend, drecv, d_ssem.at[0], d_rsem.at[0])
+            drecv[me] = dsend[...]
         to_peers(lambda k: isend.at[g, k], irecv.at[g], i_ssem.at[g], i_rsem.at[g])
         irecv[g, me] = isend[g, me]
 
@@ -521,24 +531,28 @@
 
     def leave(g, s, n):
         acc = raw_a if n < 2 else raw_b
-        at = (n % 2) * 256
+        at = (n % 2) * 2
         part = dot(nbs[s][...], wout[g * GC : (g + 1) * GC, n * 256 : (n + 1) * 256])
-        if g > 0:
-            part = part + acc[s, 0:steps, at : at + 256]
-        if g < GROUPS - 1:
-            acc[s, 0:steps, at : at + 256] = part
-            return
         for j in range(2):
-            res = part[:, j * 128 : (j + 1) * 128] * ssq[s * steps : (s + 1) * steps, :]
-            lo = n * 256 + j * 128
-            out_ref[s, :, lo : lo + 128] = res.astype(BF16)
+            piece = part[:, j * 128 : (j + 1) * 128]
+            if g > 0:
+                piece = piece + acc[s, at + j, 0:steps, :]
+            if g < GROUPS - 1:
+                acc[s, at + j, 0:steps, :] = piece
+            else:
+                lo = n * 256 + j * 128
+                res = piece * ssq[s * steps : (s + 1) * steps, :]
+                out_ref[s, :, lo : lo + 128] = res.astype(BF16)
 
     for g in range(GROUPS):
+        if g == GROUPS - 1:
+            for c in range(chunks):
+                leave(g - 1, 1, c)
         scoped("arrive", arrive, g)
         with jax.named_scope("final"):
             for c in range(chunks):
                 mix(g, 0, c)
-                if g > 0:
+                if 0 < g < GROUPS - 1:
                     leave(g - 1, 1, c)
             if g == GROUPS - 1:
                 row_scale(0)
@@ -594,8 +608,8 @@
         pltpu.VMEM((DI, D), BF16),
         pltpu.VMEM((series_here, steps, W_IN), BF16),
         pltpu.VMEM((nc, N, Q), BF16),
-        pltpu.VMEM((series_here, RIM + steps, GC), F32),
-        pltpu.VMEM((series_here, RIM + steps, GC), F32),
+        pltpu.VMEM((series_here, GC // 128, RIM + steps, 128), F32),
+        pltpu.VMEM((series_here, GC // 128, RIM + steps, 128), F32),
         pltpu.VMEM((nc, Q, 128), F32),
         pltpu.VMEM((nc, H, Q), F32),
         pltpu.VMEM((nc, Q, Q), F32),

time: 48.6 us -> 46.6 us (0.959); the launches traced: 48.5 us -> 46 us
  Pallas kernels: 47.1 us -> 44.7 us
    pallas_call x1, Pallas kernels: 47.1 us -> 44.7 us  [body(): pl.pallas_call(functools.partial(kernel, n_tm, n_ser, series_here, steps)...]
where the time goes in v4:
time: 46.6 us; the launch traced here: 46 us
  Pallas kernels  44.7 us (96%)
  local copies, waits for them, and re-layouts  1.32 us (3%)
    pallas_call x1, Pallas kernels, body(): pl.pallas_call(functools.partial(kernel, n_tm, n_ser, series_here, steps)...  44.7 us
    unnamed x1, local copies, waits for them, and re-layouts  1.32 us

profile of v4, /device:TPU:1, one launch (start us, length us, event | category | flops | bytes accessed | tf_op | source)
XLA Modules:
  0.0 46.0 jit_solution(9408605329641784748)
XLA Ops:
  0.0 44.7 %mixer.1 = bf16[2,512,1024]{2,1,0:T(8,128)(2,1)S(1)} custom-call(bf16[2,512,1024]{2,1,0:T(8,128)(2,1)} %tokens_hbm.1, bf16[1024,2048]{1,0:T(8,128)(2,1)} %gate_hbm.1, bf16[1024,2304]{1,0:T(8,128)(2,1)} %in_hbm.1, bf16[32,1024]{1,0:T(8,128)(2,1)} %bitcast.1, f32[4,2304]{1,0:T(4,128)} %convk_ref.1, f32[2304]{0:T(1024)} %convb_ref.1, f32[32]{0:T(128)} %stepb_ref.1, ...), custom_call_target="tpu_custom_call" | custom-call | tf_op jit(solution)/shard_map/mixer/pallas_call | solution.py:651
  44.7 1.3 %copy.15 = bf16[2,512,1024]{2,1,0:T(8,128)(2,1)} copy(bf16[2,512,1024]{2,1,0:T(8,128)(2,1)S(1)} %mixer.1) | data formatting | bytes 4194304

commit v5 on v4

--- a/solution.py
+++ b/solution.py
@@ -308,7 +308,7 @@
 
     def to_peers(src, dst, ssem, rsem):
         def send(d, carry):
-            k = away(d)
+            k = away(lax.rem(7 * d, n_tm))
             pltpu.make_async_remote_copy(
                 src_ref=src(k),
                 dst_ref=dst.at[me],

time: 46.6 us -> 46.7 us (level)
  no operation moved by 1% of the time
where the time goes in v5:
time: 46.7 us; the launch traced here: 46.4 us
  Pallas kernels  45.1 us (97%)
  local copies, waits for them, and re-layouts  1.32 us (3%)
    pallas_call x1, Pallas kernels, body(): pl.pallas_call(functools.partial(kernel, n_tm, n_ser, series_here, steps)...  45.1 us
    unnamed x1, local copies, waits for them, and re-layouts  1.32 us

profile of v5, /device:TPU:1, one launch (start us, length us, event | category | flops | bytes accessed | tf_op | source)
XLA Modules:
  0.0 46.4 jit_solution(6733526413699382896)
XLA Ops:
  0.0 45.1 %mixer.1 = bf16[2,512,1024]{2,1,0:T(8,128)(2,1)S(1)} custom-call(bf16[2,512,1024]{2,1,0:T(8,128)(2,1)} %tokens_hbm.1, bf16[1024,2048]{1,0:T(8,128)(2,1)} %gate_hbm.1, bf16[1024,2304]{1,0:T(8,128)(2,1)} %in_hbm.1, bf16[32,1024]{1,0:T(8,128)(2,1)} %bitcast.1, f32[4,2304]{1,0:T(4,128)} %convk_ref.1, f32[2304]{0:T(1024)} %convb_ref.1, f32[32]{0:T(128)} %stepb_ref.1, ...), custom_call_target="tpu_custom_call" | custom-call | tf_op jit(solution)/shard_map/mixer/pallas_call | solution.py:651
  45.1 1.3 %copy.15 = bf16[2,512,1024]{2,1,0:T(8,128)(2,1)} copy(bf16[2,512,1024]{2,1,0:T(8,128)(2,1)S(1)} %mixer.1) | data formatting | bytes 4194304
